TPU v7x, 32 devices: a whole 2x2x4 slice. The times are simulated.
32 devices in a mesh: dp: 2 (over x), cy: 4 (over z), cx: 4 (over y, core).
Axes of the slice: x: 2, y: 2, z: 4, core: 2. Of those that a mesh axis runs over, the one named last changes fastest.
Arguments:
- q: bfloat16 [8192, 32, 128], P(('dp', 'cy', 'cx')), parts along dimension 0
- k: bfloat16 [8192, 8, 128], P(('dp', 'cy', 'cx')), parts along dimension 0
- v: bfloat16 [8192, 8, 128], P(('dp', 'cy', 'cx')), parts along dimension 0
Outputs:
- output: bfloat16 [8192, 32, 128], P(('dp', 'cy', 'cx')), parts along dimension 0
There are 2 independent parts. A program takes and returns all parts, laid end to end along the dimension named above; each array names one.
All inputs are finite; a program needn't handle non-finite values.
Results may differ from a plain program's by a relative error of at most 0.00303333.
Values are sent between devices in bfloat16 or wider.
A program may use at most 1 GiB of HBM per device.

v0:
```python
import jax
import jax.numpy as jnp
from jax import lax
from jax.experimental import pallas as pl
from jax.experimental.pallas import tpu as pltpu
from jax.sharding import PartitionSpec as P

MESH = pl.DeviceIdType.MESH
NEG = -1.0e30
LOG2E = 1.4426950408889634
B = 512
S = 128
HD = 128

PUMP = (
    (1, 6, 2, 5, 3, 4),
    (2, 0, 5, 3, 4, 8 + 0, 8 + 7, 8 + 2, 8 + 5, 8 + 3, 8 + 4),
    (3, 1, 4, 0, 8 + 3, 8 + 1, 8 + 4, 8 + 6, 8 + 0, 8 + 7),
    (2, 1, 0, 8 + 2, 8 + 1, 8 + 0),
)
ARRIVE = (
    (12, 17, 23, 29, 34, 40),
    (12, 12.5, 17, 23, 29, 21, 25, 35, 40, 46, 51),
    (12, 12.5, 17, 18, 23, 23.5, 29, 29.5, 34, 40),
    (12, 18, 23, 29, 34, 40),
)
FULL, DIAG, FIN, OTHER = 0, 1, 2, 3
L0, M0, H0, G0, L1, M1, H1, G1, X = range(9)
RELAY, MOVE = (OTHER, 0, 0), (OTHER, 0, 1)


def seq(group, blocks, z=None, fin=False):
    out = []
    if z is not None:
        out.append((DIAG, group, 7 if group == X else z if group % 4 < 2 else 7 - z))
    out += [(FULL, group, b) for b in blocks]
    if fin:
        out.append((FIN, group, 0))
    return out


PROGRAM = (
    seq(L0, (), 0, True) + seq(H0, (0, 1), 0) + [RELAY] + seq(L1, (), 0, True) + seq(H0, (6,)) + [MOVE]
    + seq(H0, (2,)) + seq(M0, (), 0, True) + seq(H0, (5,)) + seq(G0, (0, 1, 6, 2, 5, 3), 0) + seq(H0, (3,))
    + seq(M1, (), 0, True) + seq(G0, (4,), None, True) + seq(H0, (4,), None, True),
    seq(L0, (0,), 1, True) + seq(H0, (1, 0, 2), 1) + [RELAY] + seq(H0, (5,)) + seq(L1, (), 1) + seq(H1, (1,), 1)
    + seq(L1, (0,), None, True) + seq(H1, (0,)) + seq(H0, (3,)) + seq(M0, (0,), 1, True)
    + seq(G0, (1, 0, 2, 5, 3, 4), 1, True) + seq(H0, (4,), None, True) + seq(M1, (0,), 1, True)
    + seq(X, (6, 1, 0), 1) + seq(G1, (1, 0, 2, 5), 1) + seq(H1, (2, 5)) + seq(X, (2, 5)) + seq(G1, (3,))
    + seq(H1, (3,)) + seq(X, (3,)) + seq(G1, (4,), None, True) + seq(X, (4,), None, True) + seq(H1, (4,), None, True),
    seq(L0, (1,), 2) + seq(H0, (2, 1, 3), 2) + [RELAY] + seq(L0, (0,), None, True) + seq(H0, (4, 0), None, True)
    + seq(L1, (), 2) + seq(H1, (2,), 2) + seq(M0, (1, 0), 2, True) + seq(H1, (3, 1)) + seq(L1, (1,))
    + seq(G0, (2, 1, 3, 4, 0), 2, True) + seq(H1, (4,)) + seq(M1, (1, 0), 2, True) + seq(L1, (0,), None, True)
    + seq(H1, (0,), None, True) + seq(G1, (2, 1, 3, 4, 0), 2, True) + seq(X, (5, 6, 2, 1, 3, 4, 0), 2, True),
    seq(L0, (2,), 3) + seq(H0, (3, 2), 3) + [RELAY] + seq(L0, (1,)) + seq(H0, (1,)) + seq(L1, (), 3)
    + seq(H1, (3,), 3) + seq(L0, (0,), None, True) + seq(H0, (0,), None, True) + seq(M0, (2, 1, 0), 3, True)
    + seq(G0, (3, 2, 1, 0), 3, True) + seq(L1, (2,)) + seq(H1, (2,)) + seq(M1, (2, 1), 3) + seq(L1, (1,))
    + seq(H1, (1,)) + seq(G1, (3, 2, 1), 3) + seq(M1, (0,), None, True) + seq(G1, (0,), None, True)
    + seq(L1, (0,), None, True) + seq(H1, (0,), None, True),
)


def arrivals_taken(z):
    queries = {M0: 21.6, G0: 27, M1: 33, G1: 38, X: 30} if z else {M0: 27, G0: 33, M1: 38}
    t, taken, out = 10.6, 0, []
    for op, g, b in PROGRAM[z]:
        if op == FULL and b not in (z, 7 - z):
            code = (8 if g >= 4 else 0) + b
            n = PUMP[z].index(code)
            taken = max(taken, n + 1)
            t = max(t, ARRIVE[z][n])
        elif op == FULL and b == 7 - z and g == X:
            pass
        elif op == DIAG:
            t = max(t, queries.get(g, 0))
            if g == X:
                n = PUMP[z].index(8 + 7)
                taken = max(taken, n + 1)
                t = max(t, ARRIVE[z][n])
        elif op == OTHER:
            t = max(t, 21.6 if b else 16)
        while taken < len(PUMP[z]) and ARRIVE[z][taken] <= t:
            taken += 1
        out.append(taken)
        t += (0.75, 0.6, 0.3, 0.2)[op]
    return out


def pick(z, values):
    out = jnp.int32(values[0])
    for i in range(1, len(values)):
        out = jnp.where(z == i, jnp.int32(values[i]), out)
    return out


def words(z, seqs, bits):
    per = 31 // bits
    n = max(len(q) for q in seqs)
    return [pick(z, [sum(x << (bits * i) for i, x in enumerate(q[w:w + per])) for q in seqs])
            for w in range(0, n, per)]


def entry(table, i, bits):
    per = 31 // bits
    word = table[0]
    for w in range(1, len(table)):
        word = jnp.where(i >= per * w, table[w], word)
    return lax.shift_right_logical(word, bits * (i % per)) & ((1 << bits) - 1)


def kernel(q_ref, k_ref, v_ref, o_ref, qb, kvb, ob, mb, lb, ab,
           kv_s, kv_r, q_s, q_r, z_s, z_r, f_s, o_s, o_r, x_s, x_r, xo_s, xo_r, loc, oloc):
    dp = lax.axis_index("dp")
    z = lax.axis_index("cy")
    cx = lax.axis_index("cx")
    c = (HD ** -0.5) * LOG2E
    partners = (cx, cx + 1 - 2 * (cx % 2), (cx + 2) % 4, 3 - cx)
    first, second = z == 0, z == 1
    has_dn, has_up = z > 0, z < 3
    has_x = jnp.logical_and(z >= 1, z <= 2)

    def span_at(half, who):
        return (who if half == 0 else 3 - who) * S

    def blk(half):
        return z if half == 0 else 7 - z

    def remote(src, dst, ssem, rsem, dev):
        return pltpu.make_async_remote_copy(src, dst, ssem, rsem, device_id=dev, device_id_type=MESH)

    def kv_piece(h, half, who):
        return kvb.at[h, blk(half), :, pl.ds(span_at(half, who), S)]

    def kv_send(h, half, d):
        t = partners[d]
        for ref, n in ((k_ref, 0), (v_ref, 1)):
            remote(ref.at[2 * t + h, pl.ds(half * S, S)], kvb.at[h, blk(half), n, pl.ds(span_at(half, cx), S)],
                   kv_s.at[h, half, d - 1], kv_r.at[h, half, d - 1], (dp, z, t)).start()

    def kv_both(h, half, d):
        ref = kv_piece(h, half, partners[d])
        return remote(ref, ref, kv_s.at[h, half, d - 1], kv_r.at[h, half, d - 1], (dp, z, partners[d]))

    def rows4(ref, h, half, who):
        at = jnp.where(half == 0, who % 2, 1 - who % 2) * S
        return ref.at[pl.ds(((h * 2 + half) * 2 + who // 2) * 4, 4), pl.ds(at, S)]

    def q_piece(h, half, who):
        return rows4(qb, h, half, who)

    def q_send(h, half, d):
        t = partners[d]
        return remote(q_ref.at[pl.ds(8 * t + 4 * h, 4), pl.ds(half * S, S)], q_piece(h, half, cx),
                      q_s.at[h, half, d - 1], q_r.at[h, half, d - 1], (dp, z, t))

    def q_both(h, half, d):
        ref = q_piece(h, half, partners[d])
        return remote(ref, ref, q_s.at[h, half, d - 1], q_r.at[h, half, d - 1], (dp, z, partners[d]))

    def o_send(h, half, d):
        t = partners[d]
        return remote(rows4(ob, h, half, t),
                      o_ref.at[pl.ds(8 * cx + 4 * h, 4), pl.ds(half * S, S)],
                      o_s.at[h, half, d - 1], o_r.at[h, half, d - 1], (dp, z, t))

    def o_recv(h, half, d):
        t = partners[d]
        ref = o_ref.at[pl.ds(8 * t + 4 * h, 4), pl.ds(half * S, S)]
        return remote(ref, ref, o_s.at[h, half, d - 1], o_r.at[h, half, d - 1], (dp, z, t))

    def x_send(n):
        for y in (0, 1):
            remote(qb.at[pl.ds((6 + y) * 4 + 2 * n, 2)], qb.at[pl.ds(32 + 2 * y, 2)],
                   x_s.at[n], x_r.at[0], (dp, n + 1, cx)).start()

    def x_both(n):
        ref = qb.at[pl.ds(32, 4)]
        return remote(ref, ref, x_s.at[n], x_r.at[0], (dp, 0, cx))

    def xo_send(d):
        t = partners[d]
        return remote(ob.at[pl.ds(32 + 2 * (t // 2), 2), pl.ds((1 - t % 2) * S, S)],
                      o_ref.at[pl.ds(8 * cx + 2 + 2 * z, 2), pl.ds(S, S)],
                      xo_s.at[d], xo_r.at[z - 1, d], (dp, 0, t))

    def xo_recv(n, d):
        ref = o_ref.at[pl.ds(8 * partners[d] + 4 + 2 * n, 2), pl.ds(S, S)]
        return remote(ref, ref, xo_s.at[d], xo_r.at[n, d], (dp, n + 1, partners[d]))

    def z_dev(way):
        return (dp, z + 1 if way == 0 else z - 1, cx)

    def z_own(h, half, d, way):
        b = blk(half)
        if d == 0:
            for ref, n in ((k_ref, 0), (v_ref, 1)):
                remote(ref.at[2 * cx + h, pl.ds(half * S, S)], kvb.at[h, b, n, pl.ds(span_at(half, cx), S)],
                       z_s.at[h, half, d, way], z_r.at[h, b], z_dev(way)).start()
        else:
            z_piece(h, half, d, way).start()

    def z_piece(h, half, d, way):
        ref = kv_piece(h, half, partners[d])
        return remote(ref, ref, z_s.at[h, half, d, way], z_r.at[h, blk(half)], z_dev(way))

    def z_cond(h, half, way):
        if way == 0:
            return has_up if half == 0 else (z < 2 if h == 1 else None)
        return has_dn if h == 0 else z > 1

    def z_each(h, half, d, do):
        for way in (0, 1):
            cond = z_cond(h, half, way)
            if cond is not None:
                @pl.when(cond)
                def _():
                    do(h, half, d, way)

    def own_kv(h, half):
        for ref, n in ((k_ref, 0), (v_ref, 1)):
            pltpu.make_async_copy(ref.at[2 * cx + h, pl.ds(half * S, S)],
                                  kvb.at[h, blk(half), n, pl.ds(span_at(half, cx), S)], loc.at[0, h, half]).start()

    def own_kv_wait(h, half):
        ref = kv_piece(h, half, cx)
        pltpu.make_async_copy(ref, ref, loc.at[0, h, half]).wait()

    def own_q(h, half):
        return pltpu.make_async_copy(
            q_ref.at[pl.ds(8 * cx + 4 * h, 4), pl.ds(half * S, S)], q_piece(h, half, cx), loc.at[1, h, half])

    barrier = pltpu.get_barrier_semaphore()
    for n in range(1, 16):
        other = (z * 4 + cx + n) % 16
        pl.semaphore_signal(barrier, inc=1, device_id=(dp, other // 4, other % 4), device_id_type=MESH)
    pl.semaphore_wait(barrier, 15)

    for h in (0, 1):
        for half in (0, 1):
            for d in (2, 3, 1):
                kv_send(h, half, d)
            if h == 0:
                z_each(h, half, 0, z_own)

    def send_q(h, half):
        for d in (2, 3, 1):
            q_send(h, half, d).start()

    @pl.when(first)
    def _():
        send_q(1, 1)

    send_q(0, 0)
    send_q(0, 1)
    send_q(1, 0)

    @pl.when(jnp.logical_not(first))
    def _():
        send_q(1, 1)

    for h in (0, 1):
        for half in (0, 1):
            own_kv(h, half)
            own_q(h, half).start()

    def relay_own(h):
        for half in (0, 1):
            if h == 1:
                z_each(h, half, 0, z_own)
            for d in (1, 2, 3):
                kv_both(h, half, d).wait_recv()
                z_each(h, half, d, z_own)
            own_kv_wait(h, half)

    order = words(z, PUMP, 4)

    def z_fwd(h, b, way):
        ref = kvb.at[h, b]
        return remote(ref, ref, f_s.at[h, b], z_r.at[h, b], z_dev(way))

    def fwd_ways(h, b):
        from_up = jnp.logical_and(b > z, b < 7 - z)
        down = jnp.logical_and(from_up, jnp.logical_or(z > 1, jnp.logical_and(second, h == 0)))
        up = jnp.logical_or(jnp.logical_and(has_up, b < z), jnp.logical_and(second, b == 7))
        return up, down

    def pump(i, _):
        code = entry(order, i, 4)
        h, b = code // 8, code % 8
        ref = kvb.at[h, b]
        remote(ref, ref, f_s.at[h, b], z_r.at[h, b], (dp, z, partners[1])).wait_recv()
        up, down = fwd_ways(h, b)

        @pl.when(down)
        def _():
            z_fwd(h, b, 1).start()

        @pl.when(up)
        def _():
            z_fwd(h, b, 0).start()

        return 0

    def fwd_wait(i, _):
        code = entry(order, i, 4)
        h, b = code // 8, code % 8
        up, down = fwd_ways(h, b)

        @pl.when(jnp.logical_or(up, down))
        def _():
            ref = kvb.at[h, b]
            remote(ref, ref, f_s.at[h, b], z_r.at[h, b], (dp, z, partners[1])).wait_send()

        return 0

    def chain(items, kk, vv):
        def scores(it):
            tile, nk, _ = it
            return lax.dot_general(qb[tile], kk[:nk], (((1,), (1,)), ((), ())), preferred_element_type=jnp.float32)

        def value(pend):
            tile, nk, p, alpha = pend
            pv = jnp.dot(p, vv[:nk], preferred_element_type=jnp.float32)
            ab[tile] = pv if alpha is None else alpha * ab[tile] + pv

        s = scores(items[0])
        pend = None
        for n, it in enumerate(items):
            nxt = scores(items[n + 1]) if n + 1 < len(items) else None
            tile, nk, mask = it
            if mask is not None:
                s = jnp.where(mask, s, NEG)
            m = jnp.max(s, axis=1, keepdims=True)
            if mask is None:
                old = mb[tile]
                m = jnp.maximum(old, m)
                alpha = jnp.exp2((old - m) * c)
            else:
                m = jnp.broadcast_to(m, (256, HD))
                alpha = None
            mb[tile] = m
            p = jnp.exp2((s - jnp.concatenate([m] * (nk // HD), axis=1)) * c)
            tot = p[:, :HD]
            for j in range(1, nk // HD):
                tot = tot + p[:, j * HD:(j + 1) * HD]
            lb[tile] = tot if alpha is None else alpha * lb[tile] + tot
            if pend is not None:
                value(pend)
            pend = (tile, nk, p.astype(jnp.bfloat16), alpha)
            s = nxt
        value(pend)

    def full(g, h, b):
        chain([(g * 4 + t, B, None) for t in range(4)], kvb.at[h, b, 0], kvb.at[h, b, 1])

    def diag(g, h, b, lower):
        items = []
        for t, low in enumerate(lower):
            nk = 512 if low else 256
            row = lax.broadcasted_iota(jnp.int32, (256, nk), 0) + (256 if low else 0)
            mask = lax.broadcasted_iota(jnp.int32, (256, nk), 1) <= row
            items.append((g * 4 + t, nk, mask))
        chain(items, kvb.at[h, b, 0], kvb.at[h, b, 1])

    def o_own(h, half):
        return pltpu.make_async_copy(
            rows4(ob, h, half, cx),
            o_ref.at[pl.ds(8 * cx + 4 * h, 4), pl.ds(half * S, S)], oloc.at[h, half])

    relay_own(0)
    count = [len(p) for p in PROGRAM]
    ops = words(z, [[op | g << 2 | b << 6 | n << 9 for (op, g, b), n in zip(p, arrivals_taken(i))]
                    for i, p in enumerate(PROGRAM)], 13)

    def run(i, at):
        code = entry(ops, i, 13)
        op, gc, b, upto = code % 4, (code // 4) % 16, (code // 64) % 8, code // 512
        h = jnp.where(gc < 4, 0, 1)
        half = (gc // 2) % 2
        other = gc % 2
        extra = gc == X
        y = jnp.where(other == 0, cx // 2, 1 - cx // 2)
        g = jnp.where(extra, 8, gc - other + y)
        lax.fori_loop(at, upto, pump, 0)

        @pl.when(op == FULL)
        def _():
            full(g, h, b)

        @pl.when(op == DIAG)
        def _():
            lower = jnp.where(half == 0, y == 1, y == 0)

            @pl.when(extra)
            def _():
                x_both(0).wait_recv()
                diag(8, 1, 7, (True, True, False, False))

            @pl.when(jnp.logical_not(extra))
            def _():
                @pl.when(other == 0)
                def _():
                    own_q(h, half).wait()
                    q_both(h, half, 1).wait_recv()

                @pl.when(other == 1)
                def _():
                    q_both(h, half, 2).wait_recv()
                    q_both(h, half, 3).wait_recv()

                @pl.when(lower)
                def _():
                    diag(g, h, b, (True,) * 4)

                @pl.when(jnp.logical_not(lower))
                def _():
                    diag(g, h, b, (False,) * 4)

        @pl.when(op == FIN)
        def _():
            for t in range(4):
                tile = g * 4 + t
                ob[tile] = (ab[tile] / jnp.sum(lb[tile], axis=1, keepdims=True)).astype(jnp.bfloat16)

            @pl.when(extra)
            def _():
                for d in (2, 3, 1, 0):
                    xo_send(d).start()

            @pl.when(jnp.logical_not(extra))
            def _():
                @pl.when(other == 0)
                def _():
                    o_send(h, half, 1).start()
                    o_own(h, half).start()

                @pl.when(other == 1)
                def _():
                    o_send(h, half, 2).start()
                    o_send(h, half, 3).start()

        @pl.when(op == OTHER)
        def _():
            @pl.when(b == 0)
            def _():
                relay_own(1)

            @pl.when(b == 1)
            def _():
                own_q(1, 1).wait()
                for d in (1, 2, 3):
                    q_both(1, 1, d).wait_recv()
                for n in (0, 1):
                    x_send(n)

        return upto

    lax.fori_loop(0, pick(z, count), run, jnp.int32(0))

    lax.fori_loop(0, pick(z, [len(p) for p in PUMP]), fwd_wait, 0)

    def z_wait(h, half, d, way):
        z_piece(h, half, d, way).wait_send()

    for h in (0, 1):
        for half in (0, 1):
            for d in (1, 2, 3):
                kv_both(h, half, d).wait_send()
                q_send(h, half, d).wait_send()
            for d in range(4):
                z_each(h, half, d, z_wait)

            def o_wait():
                o_own(h, half).wait()
                for d in (1, 2, 3):
                    o_send(h, half, d).wait_send()
                    o_recv(h, half, d).wait_recv()

            if (h, half) == (1, 1):
                pl.when(jnp.logical_not(first))(o_wait)
            else:
                o_wait()

    @pl.when(first)
    def _():
        for n in (0, 1):
            x_both(n).wait_send()
            for d in range(4):
                xo_recv(n, d).wait_recv()

    @pl.when(has_x)
    def _():
        for d in range(4):
            xo_send(d).wait_send()


def solution(mesh):
    spec = P(("dp", "cy", "cx"))

    def local(q, k, v):
        qt, kt, vt = (x.transpose(1, 0, 2) for x in (q, k, v))
        dma = pltpu.SemaphoreType.DMA
        out = pl.pallas_call(
            kernel,
            out_shape=jax.ShapeDtypeStruct((32, 256, HD), jnp.bfloat16),
            in_specs=[pl.BlockSpec(memory_space=pl.ANY)] * 3,
            out_specs=pl.BlockSpec(memory_space=pl.ANY),
            scratch_shapes=[
                pltpu.VMEM((36, 256, HD), jnp.bfloat16),
                pltpu.VMEM((2, 8, 2, B, HD), jnp.bfloat16),
                pltpu.VMEM((36, 256, HD), jnp.bfloat16),
                pltpu.VMEM((36, 256, HD), jnp.float32),
                pltpu.VMEM((36, 256, HD), jnp.float32),
                pltpu.VMEM((36, 256, HD), jnp.float32),
                dma((2, 2, 3)), dma((2, 2, 3)),
                dma((2, 2, 3)), dma((2, 2, 3)),
                dma((2, 2, 4, 2)), dma((2, 8)), dma((2, 8)),
                dma((2, 2, 3)), dma((2, 2, 3)),
                dma((2,)), dma((1,)), dma((4,)), dma((2, 4)),
                dma((2, 2, 2)), dma((2, 2)),
            ],
            compiler_params=pltpu.CompilerParams(
                collective_id=0, has_side_effects=True, vmem_limit_bytes=60 * 1024 * 1024),
        )(qt, kt, vt)
        return out.transpose(1, 0, 2)

    return jax.shard_map(local, mesh=mesh, in_specs=(spec, spec, spec), out_specs=spec, check_vma=False)
```

profile of v0, /device:TPU:0, one launch (start us, length us, event | category | flops | bytes accessed | tf_op | source)
XLA Modules:
  0.0 92.8 jit_solution(103572588417816902)
XLA Ops:
  0.0 0.0 copy-start
  0.0 2.5 %copy_bitcast_fusion.1 = (bf16[8,256,128]{2,1,0:T(8,128)(2,1)}, bf16[8,256,128]{2,1,0:T(8,128)(2,1)}) fusion(bf16[256,8,128]{2,1,0:T(8,128)(2,1)} %param.5, bf16[256,8,128]{2,1,0:T(8,128)(2,1)} %param.4), kind=kLoop, calls=%fused_computation.1 | loop fusion | bytes 2097152 | tf_op jit(solution)/shard_map/transpose | solution.py:501
  2.5 0.0 copy-done
  2.5 2.1 %copy.11 = bf16[256,32,128]{2,0,1:T(8,128)(2,1)} copy(bf16[256,32,128]{2,1,0:T(8,128)(2,1)S(1)} %copy-done) | data formatting | bytes 4194304 | tf_op args[0]
  4.7 83.9 %shard_map.37 = bf16[32,256,128]{2,1,0:T(8,128)(2,1)} custom-call(bf16[32,256,128]{2,1,0:T(8,128)(2,1)} %bitcast.9, bf16[8,256,128]{2,1,0:T(8,128)(2,1)} %get-tuple-element.6.k_ref, bf16[8,256,128]{2,1,0:T(8,128)(2,1)} %get-tuple-element.5.v_ref), custom_call_target="tpu_custom_call" | custom-call | tf_op jit(solution)/shard_map/pallas_call | solution.py:503
  88.5 4.3 %copy.7 = bf16[256,32,128]{2,1,0:T(8,128)(2,1)} copy(bf16[256,32,128]{2,0,1:T(8,128)(2,1)} %bitcast.8) | data formatting | bytes 4194304 | tf_op jit(solution)/shard_map/transpose | solution.py:525
Async XLA Ops:
  0.0 2.5 %copy-start = (bf16[256,32,128]{2,1,0:T(8,128)(2,1)S(1)}, bf16[256,32,128]{2,1,0:T(8,128)(2,1)}, u32[]{:S(2)}) copy-start(bf16[256,32,128]{2,1,0:T(8,128)(2,1)} %param.3) | copy-start | bytes 6291460
where the time goes:
time: 92.9 us; the launch traced here: 92.8 us
  Pallas kernels  83.9 us (90%)
  local copies, waits for them, and re-layouts  8.92 us (10%)
    pallas_call x1, Pallas kernels, local(): pl.pallas_call(kernel, out_shape=jax.ShapeDtypeStruct((32, 256, HD), jnp....  83.9 us
    transpose x1, local copies, waits for them, and re-layouts, local(): return out.transpose(1, 0, 2)  4.26 us
    transpose x1, local copies, waits for them, and re-layouts, local(): qt, kt, vt = (x.transpose(1, 0, 2) for x in (q, k, v))  2.53 us
    unnamed x3, local copies, waits for them, and re-layouts  2.13 us

commit v1 on v0

--- a/solution.py
+++ b/solution.py
@@ -48,7 +48,7 @@
     + seq(G0, (1, 0, 2, 5, 3, 4), 1, True) + seq(H0, (4,), None, True) + seq(M1, (0,), 1, True)
     + seq(X, (6, 1, 0), 1) + seq(G1, (1, 0, 2, 5), 1) + seq(H1, (2, 5)) + seq(X, (2, 5)) + seq(G1, (3,))
     + seq(H1, (3,)) + seq(X, (3,)) + seq(G1, (4,), None, True) + seq(X, (4,), None, True) + seq(H1, (4,), None, True),
-    seq(L0, (1,), 2) + seq(H0, (2, 1, 3), 2) + [RELAY] + seq(L0, (0,), None, True) + seq(H0, (4, 0), None, True)
+    seq(L0, (1,), 2) + seq(H0, (2, 1, 3), 2) + seq(L0, (0,), None, True) + seq(H0, (4,)) + [RELAY] + seq(H0, (0,), None, True)
     + seq(L1, (), 2) + seq(H1, (2,), 2) + seq(M0, (1, 0), 2, True) + seq(H1, (3, 1)) + seq(L1, (1,))
     + seq(G0, (2, 1, 3, 4, 0), 2, True) + seq(H1, (4,)) + seq(M1, (1, 0), 2, True) + seq(L1, (0,), None, True)
     + seq(H1, (0,), None, True) + seq(G1, (2, 1, 3, 4, 0), 2, True) + seq(X, (5, 6, 2, 1, 3, 4, 0), 2, True),
@@ -82,7 +82,7 @@
         while taken < len(PUMP[z]) and ARRIVE[z][taken] <= t:
             taken += 1
         out.append(taken)
-        t += (0.75, 0.6, 0.3, 0.2)[op]
+        t += (0.9, 0.8, 0.5, 0.2)[op]
     return out
 
 

time: 92.9 us -> 87.2 us (0.939)
  Pallas kernels: 83.9 us -> 78.1 us
    pallas_call x1, Pallas kernels: 83.9 us -> 78.1 us  [local(): pl.pallas_call(kernel, out_shape=jax.ShapeDtypeStruct((32, 256, HD), jnp....]
where the time goes in v1:
time: 87.2 us; the launch traced here: 87.1 us
  Pallas kernels  78.1 us (90%)
  local copies, waits for them, and re-layouts  8.92 us (10%)
    pallas_call x1, Pallas kernels, local(): pl.pallas_call(kernel, out_shape=jax.ShapeDtypeStruct((32, 256, HD), jnp....  78.1 us
    transpose x1, local copies, waits for them, and re-layouts, local(): return out.transpose(1, 0, 2)  4.26 us
    transpose x1, local copies, waits for them, and re-layouts, local(): qt, kt, vt = (x.transpose(1, 0, 2) for x in (q, k, v))  2.53 us
    unnamed x3, local copies, waits for them, and re-layouts  2.13 us

profile of v1, /device:TPU:0, one launch (start us, length us, event | category | flops | bytes accessed | tf_op | source)
XLA Modules:
  0.0 87.1 jit_solution(5222283043924734971)
XLA Ops:
  0.0 0.0 copy-start
  0.0 2.5 %copy_bitcast_fusion.1 = (bf16[8,256,128]{2,1,0:T(8,128)(2,1)}, bf16[8,256,128]{2,1,0:T(8,128)(2,1)}) fusion(bf16[256,8,128]{2,1,0:T(8,128)(2,1)} %param.5, bf16[256,8,128]{2,1,0:T(8,128)(2,1)} %param.4), kind=kLoop, calls=%fused_computation.1 | loop fusion | bytes 2097152 | tf_op jit(solution)/shard_map/transpose | solution.py:501
  2.5 0.0 copy-done
  2.5 2.1 %copy.11 = bf16[256,32,128]{2,0,1:T(8,128)(2,1)} copy(bf16[256,32,128]{2,1,0:T(8,128)(2,1)S(1)} %copy-done) | data formatting | bytes 4194304 | tf_op args[0]
  4.7 78.1 %shard_map.37 = bf16[32,256,128]{2,1,0:T(8,128)(2,1)} custom-call(bf16[32,256,128]{2,1,0:T(8,128)(2,1)} %bitcast.9, bf16[8,256,128]{2,1,0:T(8,128)(2,1)} %get-tuple-element.6.k_ref, bf16[8,256,128]{2,1,0:T(8,128)(2,1)} %get-tuple-element.5.v_ref), custom_call_target="tpu_custom_call" | custom-call | tf_op jit(solution)/shard_map/pallas_call | solution.py:503
  82.8 4.3 %copy.7 = bf16[256,32,128]{2,1,0:T(8,128)(2,1)} copy(bf16[256,32,128]{2,0,1:T(8,128)(2,1)} %bitcast.8) | data formatting | bytes 4194304 | tf_op jit(solution)/shard_map/transpose | solution.py:525
Async XLA Ops:
  0.0 2.5 %copy-start = (bf16[256,32,128]{2,1,0:T(8,128)(2,1)S(1)}, bf16[256,32,128]{2,1,0:T(8,128)(2,1)}, u32[]{:S(2)}) copy-start(bf16[256,32,128]{2,1,0:T(8,128)(2,1)} %param.3) | copy-start | bytes 6291460

commit v2 on v1

--- a/solution.py
+++ b/solution.py
@@ -13,77 +13,41 @@
 HD = 128
 
 PUMP = (
-    (1, 6, 2, 5, 3, 4),
-    (2, 0, 5, 3, 4, 8 + 0, 8 + 7, 8 + 2, 8 + 5, 8 + 3, 8 + 4),
-    (3, 1, 4, 0, 8 + 3, 8 + 1, 8 + 4, 8 + 6, 8 + 0, 8 + 7),
-    (2, 1, 0, 8 + 2, 8 + 1, 8 + 0),
+    (1, 6, 2, 5, 3, 4,),
+    (0, 2, 5, 3, 8, 4, 10, 13, 15, 11, 12,),
+    (1, 3, 4, 0, 11, 9, 12, 8, 14, 15,),
+    (2, 1, 10, 0, 9, 8,),
 )
-ARRIVE = (
-    (12, 17, 23, 29, 34, 40),
-    (12, 12.5, 17, 23, 29, 21, 25, 35, 40, 46, 51),
-    (12, 12.5, 17, 18, 23, 23.5, 29, 29.5, 34, 40),
-    (12, 18, 23, 29, 34, 40),
+FULL, DIAG, FIN, OTHER, PAIR, TRIO = range(6)
+L0, M0, H0, G0, L1, M1, H1, G1, X = range(9)
+PROGRAM = (
+    ((1, 0, 0, 0), (2, 0, 0, 0), (1, 2, 7, 0), (0, 2, 1, 1), (0, 2, 0, 1), (3, 0, 0, 2), (1, 4, 0, 2),
+     (2, 4, 0, 2), (0, 2, 6, 2), (3, 0, 1, 3), (3, 0, 2, 3), (0, 2, 2, 3), (1, 1, 0, 4), (2, 1, 0, 4),
+     (0, 2, 5, 4), (1, 3, 7, 5), (0, 3, 1, 5), (0, 3, 2, 5), (4, 2, 3, 5), (0, 3, 5, 5), (0, 3, 6, 5),
+     (4, 2, 4, 6), (0, 3, 0, 6), (2, 3, 0, 6), (2, 2, 0, 6), (1, 5, 0, 6), (2, 5, 0, 6),),
+    ((1, 0, 1, 0), (1, 2, 6, 0), (0, 0, 0, 1), (2, 0, 0, 2), (0, 2, 0, 2), (0, 2, 2, 2), (0, 2, 1, 2),
+     (3, 0, 0, 3), (1, 4, 1, 3), (1, 6, 6, 3), (0, 6, 1, 3), (0, 2, 5, 3), (1, 1, 1, 4), (0, 1, 0, 4),
+     (2, 1, 0, 4), (0, 2, 3, 4), (3, 0, 2, 5), (0, 4, 0, 5), (2, 4, 0, 5), (0, 6, 0, 5), (1, 3, 6, 6),
+     (0, 3, 0, 6), (0, 3, 2, 6), (0, 3, 3, 6), (4, 2, 4, 6), (0, 3, 5, 6), (1, 5, 1, 7), (0, 5, 0, 7),
+     (2, 5, 0, 7), (0, 6, 2, 7), (0, 3, 1, 7), (2, 3, 0, 7), (2, 2, 0, 7), (0, 6, 5, 8), (1, 7, 6, 8),
+     (0, 7, 0, 8), (3, 0, 3, 9), (0, 8, 0, 9), (0, 8, 2, 9), (0, 8, 5, 9), (5, 6, 3, 10), (1, 8, 7, 10),
+     (0, 8, 1, 10), (0, 8, 6, 10), (0, 7, 2, 10), (5, 6, 4, 11), (2, 8, 0, 11), (2, 6, 0, 11), (0, 7, 5, 11),
+     (0, 7, 1, 11), (2, 7, 0, 11),),
+    ((1, 0, 2, 0), (1, 2, 5, 0), (0, 0, 1, 1), (0, 2, 1, 2), (0, 2, 3, 2), (0, 2, 2, 2), (3, 0, 0, 3),
+     (1, 6, 5, 3), (0, 6, 2, 3), (0, 2, 4, 3), (1, 4, 2, 3), (0, 0, 0, 4), (2, 0, 0, 4), (0, 2, 0, 4),
+     (1, 1, 2, 4), (0, 1, 0, 4), (0, 1, 1, 4), (0, 6, 3, 5), (0, 6, 1, 6), (2, 1, 0, 6), (2, 2, 0, 6),
+     (0, 4, 1, 6), (1, 3, 5, 6), (0, 3, 0, 6), (0, 6, 4, 7), (0, 3, 1, 7), (0, 3, 3, 7), (1, 5, 2, 7),
+     (0, 5, 1, 7), (0, 3, 4, 7), (0, 3, 2, 7), (0, 6, 0, 8), (2, 6, 0, 8), (4, 4, 0, 8), (2, 5, 0, 8),
+     (1, 7, 5, 8), (0, 7, 0, 8), (0, 7, 1, 9), (0, 7, 3, 9), (0, 7, 4, 9), (0, 7, 2, 9), (2, 7, 0, 9),
+     (2, 4, 0, 9), (2, 3, 0, 9), (3, 0, 3, 10), (0, 8, 0, 10), (0, 8, 1, 10), (0, 8, 3, 10), (0, 8, 4, 10),
+     (0, 8, 6, 10), (1, 8, 7, 10), (0, 8, 2, 10), (0, 8, 5, 10), (2, 8, 0, 10),),
+    ((1, 0, 3, 0), (1, 2, 4, 0), (0, 0, 2, 1), (0, 2, 2, 1), (0, 2, 3, 1), (3, 0, 0, 1), (1, 6, 4, 1),
+     (0, 6, 3, 1), (1, 4, 3, 1), (0, 0, 1, 2), (0, 2, 1, 2), (1, 1, 3, 2), (0, 1, 1, 2), (0, 1, 2, 2),
+     (0, 6, 2, 3), (0, 4, 2, 3), (1, 3, 4, 3), (0, 3, 1, 3), (0, 3, 2, 3), (0, 3, 3, 3), (4, 0, 0, 4),
+     (2, 0, 0, 4), (4, 2, 0, 4), (2, 2, 0, 4), (2, 1, 0, 4), (2, 3, 0, 4), (1, 5, 3, 4), (0, 6, 1, 5),
+     (4, 4, 1, 5), (1, 7, 4, 5), (0, 7, 1, 5), (0, 7, 2, 5), (0, 7, 3, 5), (0, 5, 2, 5), (4, 6, 0, 6),
+     (2, 6, 0, 6), (2, 7, 0, 6), (4, 4, 0, 6), (2, 4, 0, 6), (2, 5, 0, 6),),
 )
-FULL, DIAG, FIN, OTHER = 0, 1, 2, 3
-L0, M0, H0, G0, L1, M1, H1, G1, X = range(9)
-RELAY, MOVE = (OTHER, 0, 0), (OTHER, 0, 1)
-
-
-def seq(group, blocks, z=None, fin=False):
-    out = []
-    if z is not None:
-        out.append((DIAG, group, 7 if group == X else z if group % 4 < 2 else 7 - z))
-    out += [(FULL, group, b) for b in blocks]
-    if fin:
-        out.append((FIN, group, 0))
-    return out
-
-
-PROGRAM = (
-    seq(L0, (), 0, True) + seq(H0, (0, 1), 0) + [RELAY] + seq(L1, (), 0, True) + seq(H0, (6,)) + [MOVE]
-    + seq(H0, (2,)) + seq(M0, (), 0, True) + seq(H0, (5,)) + seq(G0, (0, 1, 6, 2, 5, 3), 0) + seq(H0, (3,))
-    + seq(M1, (), 0, True) + seq(G0, (4,), None, True) + seq(H0, (4,), None, True),
-    seq(L0, (0,), 1, True) + seq(H0, (1, 0, 2), 1) + [RELAY] + seq(H0, (5,)) + seq(L1, (), 1) + seq(H1, (1,), 1)
-    + seq(L1, (0,), None, True) + seq(H1, (0,)) + seq(H0, (3,)) + seq(M0, (0,), 1, True)
-    + seq(G0, (1, 0, 2, 5, 3, 4), 1, True) + seq(H0, (4,), None, True) + seq(M1, (0,), 1, True)
-    + seq(X, (6, 1, 0), 1) + seq(G1, (1, 0, 2, 5), 1) + seq(H1, (2, 5)) + seq(X, (2, 5)) + seq(G1, (3,))
-    + seq(H1, (3,)) + seq(X, (3,)) + seq(G1, (4,), None, True) + seq(X, (4,), None, True) + seq(H1, (4,), None, True),
-    seq(L0, (1,), 2) + seq(H0, (2, 1, 3), 2) + seq(L0, (0,), None, True) + seq(H0, (4,)) + [RELAY] + seq(H0, (0,), None, True)
-    + seq(L1, (), 2) + seq(H1, (2,), 2) + seq(M0, (1, 0), 2, True) + seq(H1, (3, 1)) + seq(L1, (1,))
-    + seq(G0, (2, 1, 3, 4, 0), 2, True) + seq(H1, (4,)) + seq(M1, (1, 0), 2, True) + seq(L1, (0,), None, True)
-    + seq(H1, (0,), None, True) + seq(G1, (2, 1, 3, 4, 0), 2, True) + seq(X, (5, 6, 2, 1, 3, 4, 0), 2, True),
-    seq(L0, (2,), 3) + seq(H0, (3, 2), 3) + [RELAY] + seq(L0, (1,)) + seq(H0, (1,)) + seq(L1, (), 3)
-    + seq(H1, (3,), 3) + seq(L0, (0,), None, True) + seq(H0, (0,), None, True) + seq(M0, (2, 1, 0), 3, True)
-    + seq(G0, (3, 2, 1, 0), 3, True) + seq(L1, (2,)) + seq(H1, (2,)) + seq(M1, (2, 1), 3) + seq(L1, (1,))
-    + seq(H1, (1,)) + seq(G1, (3, 2, 1), 3) + seq(M1, (0,), None, True) + seq(G1, (0,), None, True)
-    + seq(L1, (0,), None, True) + seq(H1, (0,), None, True),
-)
-
-
-def arrivals_taken(z):
-    queries = {M0: 21.6, G0: 27, M1: 33, G1: 38, X: 30} if z else {M0: 27, G0: 33, M1: 38}
-    t, taken, out = 10.6, 0, []
-    for op, g, b in PROGRAM[z]:
-        if op == FULL and b not in (z, 7 - z):
-            code = (8 if g >= 4 else 0) + b
-            n = PUMP[z].index(code)
-            taken = max(taken, n + 1)
-            t = max(t, ARRIVE[z][n])
-        elif op == FULL and b == 7 - z and g == X:
-            pass
-        elif op == DIAG:
-            t = max(t, queries.get(g, 0))
-            if g == X:
-                n = PUMP[z].index(8 + 7)
-                taken = max(taken, n + 1)
-                t = max(t, ARRIVE[z][n])
-        elif op == OTHER:
-            t = max(t, 21.6 if b else 16)
-        while taken < len(PUMP[z]) and ARRIVE[z][taken] <= t:
-            taken += 1
-        out.append(taken)
-        t += (0.9, 0.8, 0.5, 0.2)[op]
-    return out
 
 
 def pick(z, values):
@@ -108,7 +72,7 @@
     return lax.shift_right_logical(word, bits * (i % per)) & ((1 << bits) - 1)
 
 
-def kernel(q_ref, k_ref, v_ref, o_ref, qb, kvb, ob, mb, lb, ab,
+def kernel(q_in, k_in, v_in, o_ref, q_raw, k_raw, v_raw, q_ref, k_ref, v_ref, qb, kvb, ob, mb, lb, ab,
            kv_s, kv_r, q_s, q_r, z_s, z_r, f_s, o_s, o_r, x_s, x_r, xo_s, xo_r, loc, oloc):
     dp = lax.axis_index("dp")
     z = lax.axis_index("cy")
@@ -205,7 +169,7 @@
 
     def z_cond(h, half, way):
         if way == 0:
-            return has_up if half == 0 else (z < 2 if h == 1 else None)
+            return has_up if half == 0 else None
         return has_dn if h == 0 else z > 1
 
     def z_each(h, half, d, do):
@@ -218,21 +182,25 @@
 
     def own_kv(h, half):
         for ref, n in ((k_ref, 0), (v_ref, 1)):
-            pltpu.make_async_copy(ref.at[2 * cx + h, pl.ds(half * S, S)],
-                                  kvb.at[h, blk(half), n, pl.ds(span_at(half, cx), S)], loc.at[0, h, half]).start()
-
-    def own_kv_wait(h, half):
-        ref = kv_piece(h, half, cx)
-        pltpu.make_async_copy(ref, ref, loc.at[0, h, half]).wait()
+            kvb[h, blk(half), n, pl.ds(span_at(half, cx), S)] = ref[2 * cx + h, half * S:(half + 1) * S]
 
     def own_q(h, half):
-        return pltpu.make_async_copy(
-            q_ref.at[pl.ds(8 * cx + 4 * h, 4), pl.ds(half * S, S)], q_piece(h, half, cx), loc.at[1, h, half])
+        at = (cx % 2 if half == 0 else 1 - cx % 2) * S
+        for t in range(4):
+            qb[((h * 2 + half) * 2 + cx // 2) * 4 + t, pl.ds(at, S)] = q_ref[8 * cx + 4 * h + t, half * S:(half + 1) * S]
+
+    loads = [pltpu.make_async_copy(src, dst, loc.at[n])
+             for n, (src, dst) in enumerate(((k_in, k_raw), (v_in, v_raw), (q_in, q_raw)))]
+    for copy in loads:
+        copy.start()
 
     barrier = pltpu.get_barrier_semaphore()
     for n in range(1, 16):
         other = (z * 4 + cx + n) % 16
         pl.semaphore_signal(barrier, inc=1, device_id=(dp, other // 4, other % 4), device_id_type=MESH)
+    for copy, src, dst in zip(loads[:2], (k_raw, v_raw), (k_ref, v_ref)):
+        copy.wait()
+        dst[...] = jnp.swapaxes(src[...], 0, 1)
     pl.semaphore_wait(barrier, 15)
 
     for h in (0, 1):
@@ -242,6 +210,13 @@
             if h == 0:
                 z_each(h, half, 0, z_own)
 
+    for h in (0, 1):
+        for half in (0, 1):
+            own_kv(h, half)
+    loads[2].wait()
+    for n in range(4):
+        q_ref[8 * n:8 * n + 8] = jnp.swapaxes(q_raw[:, 8 * n:8 * n + 8], 0, 1)
+
     def send_q(h, half):
         for d in (2, 3, 1):
             q_send(h, half, d).start()
@@ -260,8 +235,7 @@
 
     for h in (0, 1):
         for half in (0, 1):
-            own_kv(h, half)
-            own_q(h, half).start()
+            own_q(h, half)
 
     def relay_own(h):
         for half in (0, 1):
@@ -270,7 +244,6 @@
             for d in (1, 2, 3):
                 kv_both(h, half, d).wait_recv()
                 z_each(h, half, d, z_own)
-            own_kv_wait(h, half)
 
     order = words(z, PUMP, 4)
 
@@ -315,7 +288,7 @@
 
     def chain(items, kk, vv):
         def scores(it):
-            tile, nk, _ = it
+            tile, nk, _, _ = it
             return lax.dot_general(qb[tile], kk[:nk], (((1,), (1,)), ((), ())), preferred_element_type=jnp.float32)
 
         def value(pend):
@@ -327,39 +300,39 @@
         pend = None
         for n, it in enumerate(items):
             nxt = scores(items[n + 1]) if n + 1 < len(items) else None
-            tile, nk, mask = it
+            tile, nk, mask, begins = it
             if mask is not None:
                 s = jnp.where(mask, s, NEG)
             m = jnp.max(s, axis=1, keepdims=True)
-            if mask is None:
+            if begins:
+                m = jnp.broadcast_to(m, (256, HD))
+                alpha = None
+            else:
                 old = mb[tile]
                 m = jnp.maximum(old, m)
                 alpha = jnp.exp2((old - m) * c)
-            else:
-                m = jnp.broadcast_to(m, (256, HD))
-                alpha = None
             mb[tile] = m
             p = jnp.exp2((s - jnp.concatenate([m] * (nk // HD), axis=1)) * c)
             tot = p[:, :HD]
             for j in range(1, nk // HD):
                 tot = tot + p[:, j * HD:(j + 1) * HD]
-            lb[tile] = tot if alpha is None else alpha * lb[tile] + tot
+            lb[tile] = tot if begins else alpha * lb[tile] + tot
             if pend is not None:
                 value(pend)
             pend = (tile, nk, p.astype(jnp.bfloat16), alpha)
             s = nxt
         value(pend)
 
-    def full(g, h, b):
-        chain([(g * 4 + t, B, None) for t in range(4)], kvb.at[h, b, 0], kvb.at[h, b, 1])
-
-    def diag(g, h, b, lower):
+    def full(g, n, h, b):
+        chain([(g * 4 + t, B, None, False) for t in range(n)], kvb.at[h, b, 0], kvb.at[h, b, 1])
+
+    def diag(g, h, b, lower, begins):
         items = []
         for t, low in enumerate(lower):
             nk = 512 if low else 256
             row = lax.broadcasted_iota(jnp.int32, (256, nk), 0) + (256 if low else 0)
             mask = lax.broadcasted_iota(jnp.int32, (256, nk), 1) <= row
-            items.append((g * 4 + t, nk, mask))
+            items.append((g * 4 + t, nk, mask, begins))
         chain(items, kvb.at[h, b, 0], kvb.at[h, b, 1])
 
     def o_own(h, half):
@@ -367,14 +340,17 @@
             rows4(ob, h, half, cx),
             o_ref.at[pl.ds(8 * cx + 4 * h, 4), pl.ds(half * S, S)], oloc.at[h, half])
 
+    for t in range(32, 36):
+        mb[t] = jnp.full((256, HD), NEG, jnp.float32)
+        lb[t] = jnp.zeros((256, HD), jnp.float32)
+        ab[t] = jnp.zeros((256, HD), jnp.float32)
     relay_own(0)
     count = [len(p) for p in PROGRAM]
-    ops = words(z, [[op | g << 2 | b << 6 | n << 9 for (op, g, b), n in zip(p, arrivals_taken(i))]
-                    for i, p in enumerate(PROGRAM)], 13)
+    ops = words(z, [[op | g << 3 | b << 7 | n << 10 for op, g, b, n in p] for p in PROGRAM], 14)
 
     def run(i, at):
-        code = entry(ops, i, 13)
-        op, gc, b, upto = code % 4, (code // 4) % 16, (code // 64) % 8, code // 512
+        code = entry(ops, i, 14)
+        op, gc, b, upto = code % 8, (code // 8) % 16, (code // 128) % 8, code // 1024
         h = jnp.where(gc < 4, 0, 1)
         half = (gc // 2) % 2
         other = gc % 2
@@ -385,7 +361,15 @@
 
         @pl.when(op == FULL)
         def _():
-            full(g, h, b)
+            full(g, 4, h, b)
+
+        @pl.when(op == PAIR)
+        def _():
+            full(gc, 8, h, b)
+
+        @pl.when(op == TRIO)
+        def _():
+            full(H1, 12, 1, b)
 
         @pl.when(op == DIAG)
         def _():
@@ -393,14 +377,12 @@
 
             @pl.when(extra)
             def _():
-                x_both(0).wait_recv()
-                diag(8, 1, 7, (True, True, False, False))
+                diag(8, 1, 7, (True, True, False, False), False)
 
             @pl.when(jnp.logical_not(extra))
             def _():
                 @pl.when(other == 0)
                 def _():
-                    own_q(h, half).wait()
                     q_both(h, half, 1).wait_recv()
 
                 @pl.when(other == 1)
@@ -410,11 +392,11 @@
 
                 @pl.when(lower)
                 def _():
-                    diag(g, h, b, (True,) * 4)
+                    diag(g, h, b, (True,) * 4, True)
 
                 @pl.when(jnp.logical_not(lower))
                 def _():
-                    diag(g, h, b, (False,) * 4)
+                    diag(g, h, b, (False,) * 4, True)
 
         @pl.when(op == FIN)
         def _():
@@ -447,11 +429,19 @@
 
             @pl.when(b == 1)
             def _():
-                own_q(1, 1).wait()
                 for d in (1, 2, 3):
                     q_both(1, 1, d).wait_recv()
-                for n in (0, 1):
+                for n in (1, 0):
                     x_send(n)
+
+            @pl.when(b == 2)
+            def _():
+                for d in range(4):
+                    z_own(1, 1, d, 0)
+
+            @pl.when(b == 3)
+            def _():
+                x_both(0).wait_recv()
 
         return upto
 
@@ -469,6 +459,10 @@
                 q_send(h, half, d).wait_send()
             for d in range(4):
                 z_each(h, half, d, z_wait)
+                if (h, half) == (1, 1):
+                    @pl.when(z < 2)
+                    def _():
+                        z_wait(h, half, d, 0)
 
             def o_wait():
                 o_own(h, half).wait()
@@ -494,11 +488,15 @@
             xo_send(d).wait_send()
 
 
+def by_rows(x_ref, o_ref):
+    for n in range(4):
+        o_ref[:, 8 * n:8 * n + 8] = jnp.swapaxes(x_ref[8 * n:8 * n + 8], 0, 1)
+
+
 def solution(mesh):
     spec = P(("dp", "cy", "cx"))
 
     def local(q, k, v):
-        qt, kt, vt = (x.transpose(1, 0, 2) for x in (q, k, v))
         dma = pltpu.SemaphoreType.DMA
         out = pl.pallas_call(
             kernel,
@@ -506,6 +504,12 @@
             in_specs=[pl.BlockSpec(memory_space=pl.ANY)] * 3,
             out_specs=pl.BlockSpec(memory_space=pl.ANY),
             scratch_shapes=[
+                pltpu.VMEM((256, 32, HD), jnp.bfloat16),
+                pltpu.VMEM((256, 8, HD), jnp.bfloat16),
+                pltpu.VMEM((256, 8, HD), jnp.bfloat16),
+                pltpu.VMEM((32, 256, HD), jnp.bfloat16),
+                pltpu.VMEM((8, 256, HD), jnp.bfloat16),
+                pltpu.VMEM((8, 256, HD), jnp.bfloat16),
                 pltpu.VMEM((36, 256, HD), jnp.bfloat16),
                 pltpu.VMEM((2, 8, 2, B, HD), jnp.bfloat16),
                 pltpu.VMEM((36, 256, HD), jnp.bfloat16),
@@ -517,11 +521,17 @@
                 dma((2, 2, 4, 2)), dma((2, 8)), dma((2, 8)),
                 dma((2, 2, 3)), dma((2, 2, 3)),
                 dma((2,)), dma((1,)), dma((4,)), dma((2, 4)),
-                dma((2, 2, 2)), dma((2, 2)),
+                dma((3,)), dma((2, 2)),
             ],
             compiler_params=pltpu.CompilerParams(
                 collective_id=0, has_side_effects=True, vmem_limit_bytes=60 * 1024 * 1024),
-        )(qt, kt, vt)
-        return out.transpose(1, 0, 2)
+        )(q, k, v)
+        return pl.pallas_call(
+            by_rows,
+            grid=(2,),
+            out_shape=jax.ShapeDtypeStruct((256, 32, HD), jnp.bfloat16),
+            in_specs=[pl.BlockSpec((32, S, HD), lambda i: (0, i, 0))],
+            out_specs=pl.BlockSpec((S, 32, HD), lambda i: (i, 0, 0)),
+        )(out)
 
     return jax.shard_map(local, mesh=mesh, in_specs=(spec, spec, spec), out_specs=spec, check_vma=False)

time: 87.2 us -> 75 us (0.86)
  local copies, waits for them, and re-layouts: 8.92 us -> 0 us
  Pallas kernels: 78.1 us -> 74.4 us
    transpose x2 -> x0, local copies, waits for them, and re-layouts: 6.79 us -> none  [the longest x1 4.26 us: local(): return out.transpose(1, 0, 2)]
    pallas_call x1, Pallas kernels: 78.1 us -> 71.5 us  [local(): pl.pallas_call(kernel, out_shape=jax.ShapeDtypeStruct((32, 256, HD), jnp....]
    pallas_call x0 -> x1, Pallas kernels: none -> 2.88 us  [local(): pl.pallas_call(by_rows, grid=(2,), out_shape=jax.ShapeDtypeStruct((256, 3...]
    unnamed x3 -> x0, local copies, waits for them, and re-layouts: 2.13 us -> none
where the time goes in v2:
time: 75 us; the launch traced here: 74.4 us
  Pallas kernels  74.4 us (99%)
    pallas_call x1, Pallas kernels, local(): pl.pallas_call(kernel, out_shape=jax.ShapeDtypeStruct((32, 256, HD), jnp....  71.5 us
    pallas_call x1, Pallas kernels, local(): pl.pallas_call(by_rows, grid=(2,), out_shape=jax.ShapeDtypeStruct((256, 3...  2.88 us

profile of v2, /device:TPU:0, one launch (start us, length us, event | category | flops | bytes accessed | tf_op | source)
XLA Modules:
  0.0 74.4 jit_solution(17440893918490164147)
XLA Ops:
  0.0 71.5 %shard_map.37.x_ref = bf16[32,256,128]{2,1,0:T(8,128)(2,1)} custom-call(bf16[256,32,128]{2,1,0:T(8,128)(2,1)} %q_in.1, bf16[256,8,128]{2,1,0:T(8,128)(2,1)} %k_in.1, bf16[256,8,128]{2,1,0:T(8,128)(2,1)} %v_in.1), custom_call_target="tpu_custom_call" | custom-call | tf_op jit(solution)/shard_map/pallas_call | solution.py:501
  71.5 2.9 %shard_map.38 = bf16[256,32,128]{2,1,0:T(8,128)(2,1)} custom-call(bf16[32,256,128]{2,1,0:T(8,128)(2,1)} %shard_map.37.x_ref), custom_call_target="tpu_custom_call" | custom-call | tf_op jit(solution)/shard_map/pallas_call | solution.py:529

commit v3 on v2

--- a/solution.py
+++ b/solution.py
@@ -14,40 +14,45 @@
 
 PUMP = (
     (1, 6, 2, 5, 3, 4,),
-    (0, 2, 5, 3, 8, 4, 10, 13, 15, 11, 12,),
-    (1, 3, 4, 0, 11, 9, 12, 8, 14, 15,),
+    (0, 2, 5, 3, 8, 4, 10, 15, 13, 11, 12,),
+    (1, 3, 4, 0, 11, 9, 12, 8, 15, 14,),
     (2, 1, 10, 0, 9, 8,),
 )
-FULL, DIAG, FIN, OTHER, PAIR, TRIO = range(6)
-L0, M0, H0, G0, L1, M1, H1, G1, X = range(9)
+FULL, DIAG, FIN, OTHER, FULL2, FULL3 = range(6)
+X = 8
 PROGRAM = (
-    ((1, 0, 0, 0), (2, 0, 0, 0), (1, 2, 7, 0), (0, 2, 1, 1), (0, 2, 0, 1), (3, 0, 0, 2), (1, 4, 0, 2),
-     (2, 4, 0, 2), (0, 2, 6, 2), (3, 0, 1, 3), (3, 0, 2, 3), (0, 2, 2, 3), (1, 1, 0, 4), (2, 1, 0, 4),
-     (0, 2, 5, 4), (1, 3, 7, 5), (0, 3, 1, 5), (0, 3, 2, 5), (4, 2, 3, 5), (0, 3, 5, 5), (0, 3, 6, 5),
-     (4, 2, 4, 6), (0, 3, 0, 6), (2, 3, 0, 6), (2, 2, 0, 6), (1, 5, 0, 6), (2, 5, 0, 6),),
-    ((1, 0, 1, 0), (1, 2, 6, 0), (0, 0, 0, 1), (2, 0, 0, 2), (0, 2, 0, 2), (0, 2, 2, 2), (0, 2, 1, 2),
-     (3, 0, 0, 3), (1, 4, 1, 3), (1, 6, 6, 3), (0, 6, 1, 3), (0, 2, 5, 3), (1, 1, 1, 4), (0, 1, 0, 4),
-     (2, 1, 0, 4), (0, 2, 3, 4), (3, 0, 2, 5), (0, 4, 0, 5), (2, 4, 0, 5), (0, 6, 0, 5), (1, 3, 6, 6),
-     (0, 3, 0, 6), (0, 3, 2, 6), (0, 3, 3, 6), (4, 2, 4, 6), (0, 3, 5, 6), (1, 5, 1, 7), (0, 5, 0, 7),
-     (2, 5, 0, 7), (0, 6, 2, 7), (0, 3, 1, 7), (2, 3, 0, 7), (2, 2, 0, 7), (0, 6, 5, 8), (1, 7, 6, 8),
-     (0, 7, 0, 8), (3, 0, 3, 9), (0, 8, 0, 9), (0, 8, 2, 9), (0, 8, 5, 9), (5, 6, 3, 10), (1, 8, 7, 10),
-     (0, 8, 1, 10), (0, 8, 6, 10), (0, 7, 2, 10), (5, 6, 4, 11), (2, 8, 0, 11), (2, 6, 0, 11), (0, 7, 5, 11),
-     (0, 7, 1, 11), (2, 7, 0, 11),),
-    ((1, 0, 2, 0), (1, 2, 5, 0), (0, 0, 1, 1), (0, 2, 1, 2), (0, 2, 3, 2), (0, 2, 2, 2), (3, 0, 0, 3),
-     (1, 6, 5, 3), (0, 6, 2, 3), (0, 2, 4, 3), (1, 4, 2, 3), (0, 0, 0, 4), (2, 0, 0, 4), (0, 2, 0, 4),
-     (1, 1, 2, 4), (0, 1, 0, 4), (0, 1, 1, 4), (0, 6, 3, 5), (0, 6, 1, 6), (2, 1, 0, 6), (2, 2, 0, 6),
-     (0, 4, 1, 6), (1, 3, 5, 6), (0, 3, 0, 6), (0, 6, 4, 7), (0, 3, 1, 7), (0, 3, 3, 7), (1, 5, 2, 7),
-     (0, 5, 1, 7), (0, 3, 4, 7), (0, 3, 2, 7), (0, 6, 0, 8), (2, 6, 0, 8), (4, 4, 0, 8), (2, 5, 0, 8),
-     (1, 7, 5, 8), (0, 7, 0, 8), (0, 7, 1, 9), (0, 7, 3, 9), (0, 7, 4, 9), (0, 7, 2, 9), (2, 7, 0, 9),
-     (2, 4, 0, 9), (2, 3, 0, 9), (3, 0, 3, 10), (0, 8, 0, 10), (0, 8, 1, 10), (0, 8, 3, 10), (0, 8, 4, 10),
-     (0, 8, 6, 10), (1, 8, 7, 10), (0, 8, 2, 10), (0, 8, 5, 10), (2, 8, 0, 10),),
-    ((1, 0, 3, 0), (1, 2, 4, 0), (0, 0, 2, 1), (0, 2, 2, 1), (0, 2, 3, 1), (3, 0, 0, 1), (1, 6, 4, 1),
-     (0, 6, 3, 1), (1, 4, 3, 1), (0, 0, 1, 2), (0, 2, 1, 2), (1, 1, 3, 2), (0, 1, 1, 2), (0, 1, 2, 2),
-     (0, 6, 2, 3), (0, 4, 2, 3), (1, 3, 4, 3), (0, 3, 1, 3), (0, 3, 2, 3), (0, 3, 3, 3), (4, 0, 0, 4),
-     (2, 0, 0, 4), (4, 2, 0, 4), (2, 2, 0, 4), (2, 1, 0, 4), (2, 3, 0, 4), (1, 5, 3, 4), (0, 6, 1, 5),
-     (4, 4, 1, 5), (1, 7, 4, 5), (0, 7, 1, 5), (0, 7, 2, 5), (0, 7, 3, 5), (0, 5, 2, 5), (4, 6, 0, 6),
-     (2, 6, 0, 6), (2, 7, 0, 6), (4, 4, 0, 6), (2, 4, 0, 6), (2, 5, 0, 6),),
+    ((1, 0, 0, 0), (2, 0, 0, 0), (1, 0, 2, 7), (4, 1, 2, 1, 2, 0), (3, 2, 0, 0), (0, 2, 2, 6), (1, 2, 4, 0),
+     (2, 2, 4, 0), (3, 3, 0, 1), (3, 3, 0, 2), (0, 3, 2, 2), (1, 4, 1, 0), (2, 4, 1, 0), (0, 4, 2, 5),
+     (1, 5, 3, 7), (4, 5, 3, 1, 3, 2), (4, 5, 3, 3, 3, 5), (4, 5, 3, 6, 3, 0), (4, 6, 3, 4, 2, 3),
+     (2, 6, 3, 0), (1, 6, 5, 0), (2, 6, 5, 0), (0, 6, 2, 4), (2, 6, 2, 0),),
+    ((1, 0, 0, 1), (0, 1, 0, 0), (2, 2, 0, 0), (1, 2, 2, 6), (4, 2, 2, 0, 2, 2), (0, 2, 2, 1), (3, 3, 0, 0),
+     (0, 3, 2, 5), (1, 3, 4, 1), (1, 3, 6, 6), (0, 3, 6, 1), (1, 4, 1, 1), (4, 4, 1, 0, 2, 3), (2, 5, 1, 0),
+     (4, 5, 4, 0, 6, 0), (2, 5, 4, 0), (1, 6, 3, 6), (4, 6, 3, 0, 3, 2), (4, 6, 3, 3, 3, 4),
+     (4, 6, 3, 5, 3, 1), (2, 7, 3, 0), (1, 7, 5, 1), (4, 7, 5, 0, 2, 4), (3, 8, 0, 2), (2, 8, 5, 0),
+     (2, 8, 2, 0), (0, 8, 6, 2), (1, 9, 7, 6), (4, 9, 7, 0, 7, 2), (3, 9, 0, 3), (4, 9, 8, 0, 8, 2),
+     (4, 9, 8, 5, 8, 1), (4, 10, 8, 3, 8, 6), (1, 10, 8, 7), (4, 10, 7, 3, 7, 5), (4, 11, 8, 4, 7, 4),
+     (2, 11, 8, 0), (4, 11, 7, 1, 6, 3), (2, 11, 7, 0), (4, 11, 6, 4, 6, 5), (2, 11, 6, 0),),
+    ((1, 0, 0, 2), (0, 1, 0, 1), (1, 2, 2, 5), (4, 2, 2, 1, 2, 3), (0, 2, 2, 2), (3, 3, 0, 0), (0, 3, 2, 4),
+     (1, 3, 4, 2), (1, 3, 6, 5), (4, 4, 0, 0, 2, 0), (2, 4, 0, 0), (1, 4, 1, 2), (4, 4, 1, 0, 1, 1),
+     (2, 5, 1, 0), (2, 6, 2, 0), (4, 6, 4, 1, 6, 1), (1, 6, 3, 5), (4, 6, 3, 0, 3, 1), (4, 7, 3, 3, 3, 4),
+     (4, 7, 3, 2, 6, 3), (2, 7, 3, 0), (1, 7, 5, 2), (4, 7, 5, 1, 6, 4), (4, 8, 5, 0, 4, 0), (2, 8, 5, 0),
+     (1, 8, 7, 5), (4, 8, 7, 0, 7, 1), (4, 8, 7, 3, 7, 4), (4, 8, 7, 2, 6, 0), (3, 9, 0, 3),
+     (4, 9, 8, 0, 8, 1), (4, 9, 8, 3, 8, 4), (1, 9, 8, 7), (4, 9, 8, 2, 8, 5), (4, 10, 8, 6, 6, 2),
+     (2, 10, 8, 0), (2, 10, 7, 0), (2, 10, 4, 0), (2, 10, 6, 0),),
+    ((1, 0, 0, 3), (0, 1, 0, 2), (1, 1, 2, 4), (4, 1, 2, 2, 2, 3), (3, 1, 0, 0), (1, 1, 4, 3), (1, 1, 6, 4),
+     (0, 1, 6, 3), (4, 2, 0, 1, 2, 1), (1, 2, 1, 3), (4, 2, 1, 1, 1, 2), (4, 3, 4, 2, 6, 2), (1, 3, 3, 4),
+     (4, 3, 3, 1, 3, 2), (4, 4, 1, 0, 3, 0), (2, 4, 1, 0), (4, 4, 3, 3, 0, 0), (2, 4, 3, 0), (1, 4, 5, 3),
+     (4, 4, 5, 2, 2, 0), (4, 5, 5, 1, 4, 1), (1, 5, 7, 4), (4, 5, 7, 1, 7, 2), (4, 5, 7, 3, 6, 1),
+     (2, 5, 0, 0), (2, 5, 2, 0), (4, 6, 5, 0, 7, 0), (2, 6, 5, 0), (2, 6, 7, 0), (4, 6, 4, 0, 6, 0),
+     (2, 6, 4, 0), (2, 6, 6, 0),),
 )
+
+
+def encode(op, taken, *pairs):
+    word = op | taken << 3
+    for n in range(0, len(pairs), 2):
+        word |= (pairs[n] | pairs[n + 1] << 4) << (7 + 7 * (n // 2))
+    return word
 
 
 def pick(z, values):
@@ -286,21 +291,21 @@
 
         return 0
 
-    def chain(items, kk, vv):
+    def chain(items):
         def scores(it):
-            tile, nk, _, _ = it
-            return lax.dot_general(qb[tile], kk[:nk], (((1,), (1,)), ((), ())), preferred_element_type=jnp.float32)
+            tile, h, b, nk, _, _ = it
+            return lax.dot_general(qb[tile], kvb[h, b, 0, :nk], (((1,), (1,)), ((), ())), preferred_element_type=jnp.float32)
 
         def value(pend):
-            tile, nk, p, alpha = pend
-            pv = jnp.dot(p, vv[:nk], preferred_element_type=jnp.float32)
+            tile, h, b, nk, p, alpha = pend
+            pv = jnp.dot(p, kvb[h, b, 1, :nk], preferred_element_type=jnp.float32)
             ab[tile] = pv if alpha is None else alpha * ab[tile] + pv
 
         s = scores(items[0])
         pend = None
         for n, it in enumerate(items):
             nxt = scores(items[n + 1]) if n + 1 < len(items) else None
-            tile, nk, mask, begins = it
+            tile, h, b, nk, mask, begins = it
             if mask is not None:
                 s = jnp.where(mask, s, NEG)
             m = jnp.max(s, axis=1, keepdims=True)
@@ -319,12 +324,12 @@
             lb[tile] = tot if begins else alpha * lb[tile] + tot
             if pend is not None:
                 value(pend)
-            pend = (tile, nk, p.astype(jnp.bfloat16), alpha)
+            pend = (tile, h, b, nk, p.astype(jnp.bfloat16), alpha)
             s = nxt
         value(pend)
 
-    def full(g, n, h, b):
-        chain([(g * 4 + t, B, None, False) for t in range(n)], kvb.at[h, b, 0], kvb.at[h, b, 1])
+    def full(parts):
+        chain([(g * 4 + t, h, b, B, None, False) for g, h, b in parts for t in range(4)])
 
     def diag(g, h, b, lower, begins):
         items = []
@@ -332,8 +337,8 @@
             nk = 512 if low else 256
             row = lax.broadcasted_iota(jnp.int32, (256, nk), 0) + (256 if low else 0)
             mask = lax.broadcasted_iota(jnp.int32, (256, nk), 1) <= row
-            items.append((g * 4 + t, nk, mask, begins))
-        chain(items, kvb.at[h, b, 0], kvb.at[h, b, 1])
+            items.append((g * 4 + t, h, b, nk, mask, begins))
+        chain(items)
 
     def o_own(h, half):
         return pltpu.make_async_copy(
@@ -346,30 +351,26 @@
         ab[t] = jnp.zeros((256, HD), jnp.float32)
     relay_own(0)
     count = [len(p) for p in PROGRAM]
-    ops = words(z, [[op | g << 3 | b << 7 | n << 10 for op, g, b, n in p] for p in PROGRAM], 14)
+    ops = words(z, [[encode(*item) for item in p] for p in PROGRAM], 28)
 
     def run(i, at):
-        code = entry(ops, i, 14)
-        op, gc, b, upto = code % 8, (code // 8) % 16, (code // 128) % 8, code // 1024
-        h = jnp.where(gc < 4, 0, 1)
-        half = (gc // 2) % 2
-        other = gc % 2
-        extra = gc == X
+        code = entry(ops, i, 28)
+        op, upto = code % 8, (code // 8) % 16
+        parts = []
+        for n in range(3):
+            gc, b = (code // 128 ** (n + 1)) % 16, (code // (16 * 128 ** (n + 1))) % 8
+            y = jnp.where(gc % 2 == 0, cx // 2, 1 - cx // 2)
+            parts.append((jnp.where(gc == X, X, gc - gc % 2 + y), jnp.where(gc < 4, 0, 1), b))
+        gc, b = (code // 128) % 16, (code // 2048) % 8
+        half, other, extra = (gc // 2) % 2, gc % 2, gc == X
         y = jnp.where(other == 0, cx // 2, 1 - cx // 2)
-        g = jnp.where(extra, 8, gc - other + y)
+        g, h, _ = parts[0]
         lax.fori_loop(at, upto, pump, 0)
 
-        @pl.when(op == FULL)
-        def _():
-            full(g, 4, h, b)
-
-        @pl.when(op == PAIR)
-        def _():
-            full(gc, 8, h, b)
-
-        @pl.when(op == TRIO)
-        def _():
-            full(H1, 12, 1, b)
+        for n, name in ((1, FULL), (2, FULL2), (3, FULL3)):
+            @pl.when(op == name)
+            def _():
+                full(parts[:n])
 
         @pl.when(op == DIAG)
         def _():
@@ -431,13 +432,17 @@
             def _():
                 for d in (1, 2, 3):
                     q_both(1, 1, d).wait_recv()
-                for n in (1, 0):
+                for n in (1,):
                     x_send(n)
 
             @pl.when(b == 2)
             def _():
                 for d in range(4):
                     z_own(1, 1, d, 0)
+
+                @pl.when(first)
+                def _():
+                    x_send(0)
 
             @pl.when(b == 3)
             def _():
@@ -488,9 +493,29 @@
             xo_send(d).wait_send()
 
 
-def by_rows(x_ref, o_ref):
-    for n in range(4):
-        o_ref[:, 8 * n:8 * n + 8] = jnp.swapaxes(x_ref[8 * n:8 * n + 8], 0, 1)
+PARTS = 8
+
+
+def by_rows(x_ref, o_ref, x_in, out, in_sem, out_sem):
+    rows = 256 // PARTS
+
+    def fetch(n):
+        at = pl.ds(n * rows, rows)
+        return pltpu.make_async_copy(x_ref.at[:, at], x_in.at[n], in_sem.at[n])
+
+    def put(n):
+        at = pl.ds(n * rows, rows)
+        return pltpu.make_async_copy(out.at[at], o_ref.at[at], out_sem.at[n])
+
+    for n in range(PARTS):
+        fetch(n).start()
+    for n in range(PARTS):
+        fetch(n).wait()
+        for g in range(4):
+            out[n * rows:(n + 1) * rows, 8 * g:8 * g + 8] = jnp.swapaxes(x_in[n, 8 * g:8 * g + 8], 0, 1)
+        put(n).start()
+    for n in range(PARTS):
+        put(n).wait()
 
 
 def solution(mesh):
@@ -528,10 +553,15 @@
         )(q, k, v)
         return pl.pallas_call(
             by_rows,
-            grid=(2,),
             out_shape=jax.ShapeDtypeStruct((256, 32, HD), jnp.bfloat16),
-            in_specs=[pl.BlockSpec((32, S, HD), lambda i: (0, i, 0))],
-            out_specs=pl.BlockSpec((S, 32, HD), lambda i: (i, 0, 0)),
+            in_specs=[pl.BlockSpec(memory_space=pl.ANY)],
+            out_specs=pl.BlockSpec(memory_space=pl.ANY),
+            scratch_shapes=[
+                pltpu.VMEM((PARTS, 32, 256 // PARTS, HD), jnp.bfloat16),
+                pltpu.VMEM((256, 32, HD), jnp.bfloat16),
+                dma((PARTS,)), dma((PARTS,)),
+            ],
+            compiler_params=pltpu.CompilerParams(vmem_limit_bytes=60 * 1024 * 1024),
         )(out)
 
     return jax.shard_map(local, mesh=mesh, in_specs=(spec, spec, spec), out_specs=spec, check_vma=False)

time: 75 us -> 70.7 us (0.943)
  Pallas kernels: 74.4 us -> 70.5 us
    pallas_call x1, Pallas kernels: 71.5 us -> 68 us  [local(): pl.pallas_call(kernel, out_shape=jax.ShapeDtypeStruct((32, 256, HD), jnp....]
where the time goes in v3:
time: 70.7 us; the launch traced here: 70.5 us
  Pallas kernels  70.5 us (100%)
    pallas_call x1, Pallas kernels, local(): pl.pallas_call(kernel, out_shape=jax.ShapeDtypeStruct((32, 256, HD), jnp....  68 us
    pallas_call x1, Pallas kernels, local(): pl.pallas_call(by_rows, out_shape=jax.ShapeDtypeStruct((256, 32, HD), jnp...  2.48 us

profile of v3, /device:TPU:0, one launch (start us, length us, event | category | flops | bytes accessed | tf_op | source)
XLA Modules:
  0.0 70.5 jit_solution(17288221475242402831)
XLA Ops:
  0.0 68.0 %shard_map.37.x_ref = bf16[32,256,128]{2,1,0:T(8,128)(2,1)} custom-call(bf16[256,32,128]{2,1,0:T(8,128)(2,1)} %q_in.1, bf16[256,8,128]{2,1,0:T(8,128)(2,1)} %k_in.1, bf16[256,8,128]{2,1,0:T(8,128)(2,1)} %v_in.1), custom_call_target="tpu_custom_call" | custom-call | tf_op jit(solution)/shard_map/pallas_call | solution.py:526
  68.0 2.5 %shard_map.38 = bf16[256,32,128]{2,1,0:T(8,128)(2,1)} custom-call(bf16[32,256,128]{2,1,0:T(8,128)(2,1)} %shard_map.37.x_ref), custom_call_target="tpu_custom_call" | custom-call | tf_op jit(solution)/shard_map/pallas_call | solution.py:554

commit v4 on v3

--- a/solution.py
+++ b/solution.py
@@ -21,38 +21,20 @@
 FULL, DIAG, FIN, OTHER, FULL2, FULL3 = range(6)
 X = 8
 PROGRAM = (
-    ((1, 0, 0, 0), (2, 0, 0, 0), (1, 0, 2, 7), (4, 1, 2, 1, 2, 0), (3, 2, 0, 0), (0, 2, 2, 6), (1, 2, 4, 0),
-     (2, 2, 4, 0), (3, 3, 0, 1), (3, 3, 0, 2), (0, 3, 2, 2), (1, 4, 1, 0), (2, 4, 1, 0), (0, 4, 2, 5),
-     (1, 5, 3, 7), (4, 5, 3, 1, 3, 2), (4, 5, 3, 3, 3, 5), (4, 5, 3, 6, 3, 0), (4, 6, 3, 4, 2, 3),
-     (2, 6, 3, 0), (1, 6, 5, 0), (2, 6, 5, 0), (0, 6, 2, 4), (2, 6, 2, 0),),
-    ((1, 0, 0, 1), (0, 1, 0, 0), (2, 2, 0, 0), (1, 2, 2, 6), (4, 2, 2, 0, 2, 2), (0, 2, 2, 1), (3, 3, 0, 0),
-     (0, 3, 2, 5), (1, 3, 4, 1), (1, 3, 6, 6), (0, 3, 6, 1), (1, 4, 1, 1), (4, 4, 1, 0, 2, 3), (2, 5, 1, 0),
-     (4, 5, 4, 0, 6, 0), (2, 5, 4, 0), (1, 6, 3, 6), (4, 6, 3, 0, 3, 2), (4, 6, 3, 3, 3, 4),
-     (4, 6, 3, 5, 3, 1), (2, 7, 3, 0), (1, 7, 5, 1), (4, 7, 5, 0, 2, 4), (3, 8, 0, 2), (2, 8, 5, 0),
-     (2, 8, 2, 0), (0, 8, 6, 2), (1, 9, 7, 6), (4, 9, 7, 0, 7, 2), (3, 9, 0, 3), (4, 9, 8, 0, 8, 2),
-     (4, 9, 8, 5, 8, 1), (4, 10, 8, 3, 8, 6), (1, 10, 8, 7), (4, 10, 7, 3, 7, 5), (4, 11, 8, 4, 7, 4),
-     (2, 11, 8, 0), (4, 11, 7, 1, 6, 3), (2, 11, 7, 0), (4, 11, 6, 4, 6, 5), (2, 11, 6, 0),),
-    ((1, 0, 0, 2), (0, 1, 0, 1), (1, 2, 2, 5), (4, 2, 2, 1, 2, 3), (0, 2, 2, 2), (3, 3, 0, 0), (0, 3, 2, 4),
-     (1, 3, 4, 2), (1, 3, 6, 5), (4, 4, 0, 0, 2, 0), (2, 4, 0, 0), (1, 4, 1, 2), (4, 4, 1, 0, 1, 1),
-     (2, 5, 1, 0), (2, 6, 2, 0), (4, 6, 4, 1, 6, 1), (1, 6, 3, 5), (4, 6, 3, 0, 3, 1), (4, 7, 3, 3, 3, 4),
-     (4, 7, 3, 2, 6, 3), (2, 7, 3, 0), (1, 7, 5, 2), (4, 7, 5, 1, 6, 4), (4, 8, 5, 0, 4, 0), (2, 8, 5, 0),
-     (1, 8, 7, 5), (4, 8, 7, 0, 7, 1), (4, 8, 7, 3, 7, 4), (4, 8, 7, 2, 6, 0), (3, 9, 0, 3),
-     (4, 9, 8, 0, 8, 1), (4, 9, 8, 3, 8, 4), (1, 9, 8, 7), (4, 9, 8, 2, 8, 5), (4, 10, 8, 6, 6, 2),
-     (2, 10, 8, 0), (2, 10, 7, 0), (2, 10, 4, 0), (2, 10, 6, 0),),
-    ((1, 0, 0, 3), (0, 1, 0, 2), (1, 1, 2, 4), (4, 1, 2, 2, 2, 3), (3, 1, 0, 0), (1, 1, 4, 3), (1, 1, 6, 4),
-     (0, 1, 6, 3), (4, 2, 0, 1, 2, 1), (1, 2, 1, 3), (4, 2, 1, 1, 1, 2), (4, 3, 4, 2, 6, 2), (1, 3, 3, 4),
-     (4, 3, 3, 1, 3, 2), (4, 4, 1, 0, 3, 0), (2, 4, 1, 0), (4, 4, 3, 3, 0, 0), (2, 4, 3, 0), (1, 4, 5, 3),
-     (4, 4, 5, 2, 2, 0), (4, 5, 5, 1, 4, 1), (1, 5, 7, 4), (4, 5, 7, 1, 7, 2), (4, 5, 7, 3, 6, 1),
-     (2, 5, 0, 0), (2, 5, 2, 0), (4, 6, 5, 0, 7, 0), (2, 6, 5, 0), (2, 6, 7, 0), (4, 6, 4, 0, 6, 0),
-     (2, 6, 4, 0), (2, 6, 6, 0),),
+    (0x3901, 0x100, 0x908, 0x9, 0xa, 0x13, 0x3110, 0x211, 0x212, 0x81b, 0x101b, 0x1118, 0x2920, 0xa1, 0xa2,
+     0x1928, 0x39a9, 0x8c9ac, 0x14d9ac, 0xf1ac, 0x10e134, 0x132, 0x1b2, 0x2b1, 0x2b2,),
+    (0x801, 0x8, 0x12, 0x3111, 0x88114, 0x910, 0x1b, 0xa19, 0x2918, 0x3319, 0xb18, 0x8a1, 0xc80a4, 0xaa,
+     0x1822c, 0x22a, 0x31b1, 0x8c1b4, 0x10d9b4, 0x4e9b4, 0x1ba, 0x9a13c, 0x1043, 0x142, 0xac1, 0x2c0, 0x2ca,
+     0x33c9, 0x9c3cc, 0x184b, 0xa044c, 0x62c4c, 0x1a1c54, 0x3c51, 0x15dbd4, 0x11e45c, 0x45a, 0xd8bdc, 0x3da,
+     0x15a35c, 0x35a,),
+    (0x1001, 0x808, 0x2911, 0xc8914, 0x1110, 0x1b, 0x2118, 0x2b19, 0x1318, 0x8024, 0x22, 0x122, 0x10a1,
+     0x440a4, 0xd8b34, 0xb2, 0x29b1, 0x4c1b4, 0xce33c, 0x8e1bc, 0x12b9, 0xab8, 0x1ba, 0x182c4, 0x2c2, 0x342,
+     0x2bc1, 0x5c3c4, 0x11dbc4, 0x184b, 0x6044c, 0x121c4c, 0x3c49, 0x16144c, 0x9f454, 0x452, 0x3d2, 0x1251,
+     0x50254, 0x252,),
+    (0x1801, 0x1008, 0x2109, 0xc910c, 0xb, 0x2309, 0x1b08, 0x1a09, 0x48814, 0x1891, 0x84894, 0x9131c, 0x2199,
+     0x8c99c, 0x1998, 0xa4, 0xa2, 0x22, 0x81a4, 0x1a2, 0x50b2c, 0x12a, 0x23a9, 0x9cbac, 0x1ba8, 0x1aa9,
+     0x94aac, 0x183b4, 0x3b2, 0x332, 0x14234, 0x232, 0x2b2,),
 )
-
-
-def encode(op, taken, *pairs):
-    word = op | taken << 3
-    for n in range(0, len(pairs), 2):
-        word |= (pairs[n] | pairs[n + 1] << 4) << (7 + 7 * (n // 2))
-    return word
 
 
 def pick(z, values):
@@ -200,13 +182,23 @@
         copy.start()
 
     barrier = pltpu.get_barrier_semaphore()
+    greeted = jnp.int32(0)
     for n in range(1, 16):
         other = (z * 4 + cx + n) % 16
-        pl.semaphore_signal(barrier, inc=1, device_id=(dp, other // 4, other % 4), device_id_type=MESH)
+        oz, ox = other // 4, other % 4
+        next_to = jnp.logical_and(ox == cx, jnp.logical_or(oz == z + 1, oz == z - 1))
+        moved = jnp.logical_and(oz * z == 0, jnp.maximum(oz, z) < 3)
+        meet = jnp.logical_or(oz == z, jnp.logical_or(next_to, moved))
+        greeted += jnp.where(meet, 1, 0)
+
+        @pl.when(meet)
+        def _():
+            pl.semaphore_signal(barrier, inc=1, device_id=(dp, oz, ox), device_id_type=MESH)
+
     for copy, src, dst in zip(loads[:2], (k_raw, v_raw), (k_ref, v_ref)):
         copy.wait()
         dst[...] = jnp.swapaxes(src[...], 0, 1)
-    pl.semaphore_wait(barrier, 15)
+    pl.semaphore_wait(barrier, greeted)
 
     for h in (0, 1):
         for half in (0, 1):
@@ -351,7 +343,7 @@
         ab[t] = jnp.zeros((256, HD), jnp.float32)
     relay_own(0)
     count = [len(p) for p in PROGRAM]
-    ops = words(z, [[encode(*item) for item in p] for p in PROGRAM], 28)
+    ops = words(z, PROGRAM, 28)
 
     def run(i, at):
         code = entry(ops, i, 28)

time: 70.7 us -> 70.3 us (level)
  no operation moved by 1% of the time
where the time goes in v4:
time: 70.3 us; the launch traced here: 70.2 us
  Pallas kernels  70.1 us (100%)
    pallas_call x1, Pallas kernels, local(): pl.pallas_call(kernel, out_shape=jax.ShapeDtypeStruct((32, 256, HD), jnp....  67.7 us
    pallas_call x1, Pallas kernels, local(): pl.pallas_call(by_rows, out_shape=jax.ShapeDtypeStruct((256, 32, HD), jnp...  2.48 us

profile of v4, /device:TPU:0, one launch (start us, length us, event | category | flops | bytes accessed | tf_op | source)
XLA Modules:
  0.0 70.2 jit_solution(13210272187342411797)
XLA Ops:
  0.0 67.7 %shard_map.37.x_ref = bf16[32,256,128]{2,1,0:T(8,128)(2,1)} custom-call(bf16[256,32,128]{2,1,0:T(8,128)(2,1)} %q_in.1, bf16[256,8,128]{2,1,0:T(8,128)(2,1)} %k_in.1, bf16[256,8,128]{2,1,0:T(8,128)(2,1)} %v_in.1), custom_call_target="tpu_custom_call" | custom-call | tf_op jit(solution)/shard_map/pallas_call | solution.py:518
  67.7 2.5 %shard_map.38 = bf16[256,32,128]{2,1,0:T(8,128)(2,1)} custom-call(bf16[32,256,128]{2,1,0:T(8,128)(2,1)} %shard_map.37.x_ref), custom_call_target="tpu_custom_call" | custom-call | tf_op jit(solution)/shard_map/pallas_call | solution.py:546

commit v5 on v4

--- a/solution.py
+++ b/solution.py
@@ -13,28 +13,36 @@
 HD = 128
 
 PUMP = (
-    (1, 6, 2, 5, 3, 4,),
-    (0, 2, 5, 3, 8, 4, 10, 15, 13, 11, 12,),
-    (1, 3, 4, 0, 11, 9, 12, 8, 15, 14,),
-    (2, 1, 10, 0, 9, 8,),
+    (0x435261,),
+    (0xcbdfa483520,),
+    (0xef8c9b0431,),
+    (0x890a12,),
 )
 FULL, DIAG, FIN, OTHER, FULL2, FULL3 = range(6)
 X = 8
 PROGRAM = (
-    (0x3901, 0x100, 0x908, 0x9, 0xa, 0x13, 0x3110, 0x211, 0x212, 0x81b, 0x101b, 0x1118, 0x2920, 0xa1, 0xa2,
-     0x1928, 0x39a9, 0x8c9ac, 0x14d9ac, 0xf1ac, 0x10e134, 0x132, 0x1b2, 0x2b1, 0x2b2,),
-    (0x801, 0x8, 0x12, 0x3111, 0x88114, 0x910, 0x1b, 0xa19, 0x2918, 0x3319, 0xb18, 0x8a1, 0xc80a4, 0xaa,
-     0x1822c, 0x22a, 0x31b1, 0x8c1b4, 0x10d9b4, 0x4e9b4, 0x1ba, 0x9a13c, 0x1043, 0x142, 0xac1, 0x2c0, 0x2ca,
-     0x33c9, 0x9c3cc, 0x184b, 0xa044c, 0x62c4c, 0x1a1c54, 0x3c51, 0x15dbd4, 0x11e45c, 0x45a, 0xd8bdc, 0x3da,
-     0x15a35c, 0x35a,),
-    (0x1001, 0x808, 0x2911, 0xc8914, 0x1110, 0x1b, 0x2118, 0x2b19, 0x1318, 0x8024, 0x22, 0x122, 0x10a1,
-     0x440a4, 0xd8b34, 0xb2, 0x29b1, 0x4c1b4, 0xce33c, 0x8e1bc, 0x12b9, 0xab8, 0x1ba, 0x182c4, 0x2c2, 0x342,
-     0x2bc1, 0x5c3c4, 0x11dbc4, 0x184b, 0x6044c, 0x121c4c, 0x3c49, 0x16144c, 0x9f454, 0x452, 0x3d2, 0x1251,
-     0x50254, 0x252,),
-    (0x1801, 0x1008, 0x2109, 0xc910c, 0xb, 0x2309, 0x1b08, 0x1a09, 0x48814, 0x1891, 0x84894, 0x9131c, 0x2199,
-     0x8c99c, 0x1998, 0xa4, 0xa2, 0x22, 0x81a4, 0x1a2, 0x50b2c, 0x12a, 0x23a9, 0x9cbac, 0x1ba8, 0x1aa9,
-     0x94aac, 0x183b4, 0x3b2, 0x332, 0x14234, 0x232, 0x2b2,),
+    (0x90800001000003901, 0x13000000a0000009, 0x21200002110003110, 0x1118000101b000081b, 0xa200000a10002920,
+     0x8c9ac00039a90001928, 0x10e134000f1ac014d9ac, 0x2b100001b20000132, 0x2b2,),
+    (0x1200000080000801, 0x91000881140003111, 0x29180000a19000001b, 0x8a10000b180003319, 0x1822c00000aa00c80a4,
+     0x8c1b400031b1000022a, 0x1ba004e9b4010d9b4, 0x1420001043009a13c, 0x2ca00002c00000ac1, 0x184b009c3cc00033c9,
+     0x1a1c540062c4c00a044c, 0x11e45c015dbd40003c51, 0x3da00d8bdc000045a, 0x35a015a35c,),
+    (0x291100008080001001, 0x1b000111000c8914, 0x13180002b190002118, 0x12200000220008024, 0xd8b3400440a400010a1,
+     0x4c1b400029b100000b2, 0x12b9008e1bc00ce33c, 0x182c400001ba0000ab8, 0x2bc1000034200002c2, 0x184b011dbc4005c3c4,
+     0x3c490121c4c006044c, 0x452009f454016144c, 0x50254000125100003d2, 0x252,),
+    (0x210900010080001801, 0x2309000000b00c910c, 0x488140001a090001b08, 0x9131c00848940001891, 0x1998008c99c0002199,
+     0x2200000a200000a4, 0x50b2c00001a200081a4, 0x9cbac00023a9000012a, 0x94aac0001aa90001ba8, 0x33200003b200183b4,
+     0x2b200002320014234,),
 )
+TAKEN = (6, 11, 10, 6)
+STEPS = (25, 41, 40, 33)
+BOTH = (0, 1)
+OTHERS = (1, 2, 3)
+FAR_FIRST = (2, 3, 1)
+
+
+def unpack(rows, bits, count):
+    per = 84 // bits
+    return [[rows[i // per] >> bits * (i % per) & (1 << bits) - 1 for i in range(n)] for rows, n in zip(rows, count)]
 
 
 def pick(z, values):
@@ -120,7 +128,7 @@
         return remote(ref, ref, o_s.at[h, half, d - 1], o_r.at[h, half, d - 1], (dp, z, t))
 
     def x_send(n):
-        for y in (0, 1):
+        for y in BOTH:
             remote(qb.at[pl.ds((6 + y) * 4 + 2 * n, 2)], qb.at[pl.ds(32 + 2 * y, 2)],
                    x_s.at[n], x_r.at[0], (dp, n + 1, cx)).start()
 
@@ -160,7 +168,7 @@
         return has_dn if h == 0 else z > 1
 
     def z_each(h, half, d, do):
-        for way in (0, 1):
+        for way in BOTH:
             cond = z_cond(h, half, way)
             if cond is not None:
                 @pl.when(cond)
@@ -200,22 +208,22 @@
         dst[...] = jnp.swapaxes(src[...], 0, 1)
     pl.semaphore_wait(barrier, greeted)
 
-    for h in (0, 1):
-        for half in (0, 1):
-            for d in (2, 3, 1):
+    for h in BOTH:
+        for half in BOTH:
+            for d in FAR_FIRST:
                 kv_send(h, half, d)
             if h == 0:
                 z_each(h, half, 0, z_own)
 
-    for h in (0, 1):
-        for half in (0, 1):
+    for h in BOTH:
+        for half in BOTH:
             own_kv(h, half)
     loads[2].wait()
     for n in range(4):
         q_ref[8 * n:8 * n + 8] = jnp.swapaxes(q_raw[:, 8 * n:8 * n + 8], 0, 1)
 
     def send_q(h, half):
-        for d in (2, 3, 1):
+        for d in FAR_FIRST:
             q_send(h, half, d).start()
 
     @pl.when(first)
@@ -230,19 +238,19 @@
     def _():
         send_q(1, 1)
 
-    for h in (0, 1):
-        for half in (0, 1):
+    for h in BOTH:
+        for half in BOTH:
             own_q(h, half)
 
     def relay_own(h):
-        for half in (0, 1):
+        for half in BOTH:
             if h == 1:
                 z_each(h, half, 0, z_own)
-            for d in (1, 2, 3):
+            for d in OTHERS:
                 kv_both(h, half, d).wait_recv()
                 z_each(h, half, d, z_own)
 
-    order = words(z, PUMP, 4)
+    order = words(z, unpack(PUMP, 4, TAKEN), 4)
 
     def z_fwd(h, b, way):
         ref = kvb.at[h, b]
@@ -342,8 +350,7 @@
         lb[t] = jnp.zeros((256, HD), jnp.float32)
         ab[t] = jnp.zeros((256, HD), jnp.float32)
     relay_own(0)
-    count = [len(p) for p in PROGRAM]
-    ops = words(z, PROGRAM, 28)
+    ops = words(z, unpack(PROGRAM, 28, STEPS), 28)
 
     def run(i, at):
         code = entry(ops, i, 28)
@@ -422,7 +429,7 @@
 
             @pl.when(b == 1)
             def _():
-                for d in (1, 2, 3):
+                for d in OTHERS:
                     q_both(1, 1, d).wait_recv()
                 for n in (1,):
                     x_send(n)
@@ -442,16 +449,16 @@
 
         return upto
 
-    lax.fori_loop(0, pick(z, count), run, jnp.int32(0))
-
-    lax.fori_loop(0, pick(z, [len(p) for p in PUMP]), fwd_wait, 0)
+    lax.fori_loop(0, pick(z, STEPS), run, jnp.int32(0))
+
+    lax.fori_loop(0, pick(z, TAKEN), fwd_wait, 0)
 
     def z_wait(h, half, d, way):
         z_piece(h, half, d, way).wait_send()
 
-    for h in (0, 1):
-        for half in (0, 1):
-            for d in (1, 2, 3):
+    for h in BOTH:
+        for half in BOTH:
+            for d in OTHERS:
                 kv_both(h, half, d).wait_send()
                 q_send(h, half, d).wait_send()
             for d in range(4):
@@ -463,7 +470,7 @@
 
             def o_wait():
                 o_own(h, half).wait()
-                for d in (1, 2, 3):
+                for d in OTHERS:
                     o_send(h, half, d).wait_send()
                     o_recv(h, half, d).wait_recv()
 
@@ -474,7 +481,7 @@
 
     @pl.when(first)
     def _():
-        for n in (0, 1):
+        for n in BOTH:
             x_both(n).wait_send()
             for d in range(4):
                 xo_recv(n, d).wait_recv()

time: 70.3 us -> 70.3 us (level)
  no operation moved by 1% of the time
where the time goes in v5:
time: 70.3 us; the launch traced here: 70.2 us
  Pallas kernels  70.1 us (100%)
    pallas_call x1, Pallas kernels, local(): pl.pallas_call(kernel, out_shape=jax.ShapeDtypeStruct((32, 256, HD), jnp....  67.7 us
    pallas_call x1, Pallas kernels, local(): pl.pallas_call(by_rows, out_shape=jax.ShapeDtypeStruct((256, 32, HD), jnp...  2.48 us

profile of v5, /device:TPU:0, one launch (start us, length us, event | category | flops | bytes accessed | tf_op | source)
XLA Modules:
  0.0 70.2 jit_solution(13210272187342411797)
XLA Ops:
  0.0 67.7 %shard_map.37.x_ref = bf16[32,256,128]{2,1,0:T(8,128)(2,1)} custom-call(bf16[256,32,128]{2,1,0:T(8,128)(2,1)} %q_in.1, bf16[256,8,128]{2,1,0:T(8,128)(2,1)} %k_in.1, bf16[256,8,128]{2,1,0:T(8,128)(2,1)} %v_in.1), custom_call_target="tpu_custom_call" | custom-call | tf_op jit(solution)/shard_map/pallas_call | solution.py:525
  67.7 2.5 %shard_map.38 = bf16[256,32,128]{2,1,0:T(8,128)(2,1)} custom-call(bf16[32,256,128]{2,1,0:T(8,128)(2,1)} %shard_map.37.x_ref), custom_call_target="tpu_custom_call" | custom-call | tf_op jit(solution)/shard_map/pallas_call | solution.py:553

commit v6 on v5

--- a/solution.py
+++ b/solution.py
@@ -400,17 +400,22 @@
 
         @pl.when(op == FIN)
         def _():
-            for t in range(4):
-                tile = g * 4 + t
+            def finish(tile):
                 ob[tile] = (ab[tile] / jnp.sum(lb[tile], axis=1, keepdims=True)).astype(jnp.bfloat16)
 
             @pl.when(extra)
             def _():
-                for d in (2, 3, 1, 0):
-                    xo_send(d).start()
+                for far, targets in ((1 - cx // 2, (2, 3)), (cx // 2, (1, 0))):
+                    for t in BOTH:
+                        finish(32 + 2 * far + t)
+                    for d in targets:
+                        xo_send(d).start()
 
             @pl.when(jnp.logical_not(extra))
             def _():
+                for t in range(4):
+                    finish(g * 4 + t)
+
                 @pl.when(other == 0)
                 def _():
                     o_send(h, half, 1).start()

time: 70.3 us -> 70.2 us (level)
  no operation moved by 1% of the time
where the time goes in v6:
time: 70.2 us; the launch traced here: 70.1 us
  Pallas kernels  70.1 us (100%)
    pallas_call x1, Pallas kernels, local(): pl.pallas_call(kernel, out_shape=jax.ShapeDtypeStruct((32, 256, HD), jnp....  67.6 us
    pallas_call x1, Pallas kernels, local(): pl.pallas_call(by_rows, out_shape=jax.ShapeDtypeStruct((256, 32, HD), jnp...  2.48 us

profile of v6, /device:TPU:0, one launch (start us, length us, event | category | flops | bytes accessed | tf_op | source)
XLA Modules:
  0.0 70.1 jit_solution(17711573647951853077)
XLA Ops:
  0.0 67.6 %shard_map.37.x_ref = bf16[32,256,128]{2,1,0:T(8,128)(2,1)} custom-call(bf16[256,32,128]{2,1,0:T(8,128)(2,1)} %q_in.1, bf16[256,8,128]{2,1,0:T(8,128)(2,1)} %k_in.1, bf16[256,8,128]{2,1,0:T(8,128)(2,1)} %v_in.1), custom_call_target="tpu_custom_call" | custom-call | tf_op jit(solution)/shard_map/pallas_call | solution.py:530
  67.6 2.5 %shard_map.38 = bf16[256,32,128]{2,1,0:T(8,128)(2,1)} custom-call(bf16[32,256,128]{2,1,0:T(8,128)(2,1)} %shard_map.37.x_ref), custom_call_target="tpu_custom_call" | custom-call | tf_op jit(solution)/shard_map/pallas_call | solution.py:558
